TPU v7x, 512 devices: a whole 4x8x8 slice. The times are simulated.
512 devices in a mesh: samp: 64 (over x, z, y_lo), tgt: 8 (over y_hi, core).
Axes of the slice: x: 4, y: 8 (y_hi: 4, y_lo: 2; y = y_hi * 2 + y_lo), z: 8, core: 2. Of those that a mesh axis runs over, the one named last changes fastest.
Arguments:
- samples: bfloat16 [12288, 128], P('samp'), may hold values from -6 to 6
- omega: bfloat16 [128, 4096], replicated, may hold values from -0.5 to 0.5
- phase: float32 [4096], replicated, may hold values from -3.140625 to 3.140625
- right_side: float32 [4096, 512], P('samp', 'tgt'), may hold values from -6 to 6
Outputs:
- weights: float32 [4096, 512], P('samp', 'tgt')
All inputs are finite; a program needn't handle non-finite values.
Results may differ from a plain program's by a relative error of at most 0.011.
The roundings to bfloat16 on the way count: a program that leaves them out, or rounds other values in their place, can miss the bound.
Values may be sent and summed in bfloat16 or wider, within the bound.
A program may use at most 128 MiB of HBM per device.

v0:
```python
import math

import jax
import jax.numpy as jnp
from jax import lax
from jax.sharding import PartitionSpec as P

ITERS = 2


ridge = 1.0


def gathered_total(value, axis):
    tiles = lax.all_gather(value, axis)
    return tiles.sum(axis=0)


def laid_out(tiles, dim):
    shape = list(tiles.shape[1:])
    shape[dim] *= tiles.shape[0]
    return jnp.moveaxis(tiles, 0, dim).reshape(shape)


def sent_to_all(value, axis):
    length = lax.axis_size(axis)
    return lax.all_to_all(
        jnp.broadcast_to(value[None], (length, *value.shape)), axis, 0, 0, tiled=True
    )


def gathered_copies(value, axis, dim):
    return laid_out(sent_to_all(value, axis), dim)


def cut_along(value, dim, length):
    before, after = (value.shape[:dim], value.shape[dim + 1 :])
    return jnp.moveaxis(value.reshape(*before, length, -1, *after), dim, 0)


def sum_at_owner(value, axis, dim):
    tiles = cut_along(value, dim, lax.axis_size(axis))
    arrived = lax.all_to_all(tiles, axis, split_axis=0, concat_axis=0, tiled=True)
    return arrived.sum(axis=0)


def precise_dot(left_matrix, right_matrix):
    return jnp.dot(left_matrix, right_matrix, precision=lax.Precision.HIGHEST)


def spd_solve(gram_matrix, rhs_matrix):
    factor = jnp.linalg.cholesky(gram_matrix)
    return jax.scipy.linalg.cho_solve((factor, True), rhs_matrix)


def cosine_block(samples, omega, phase, first_row, row_count):
    omega_cols = lax.dynamic_slice_in_dim(omega, first_row, row_count, 1)
    phase_cols = lax.dynamic_slice_in_dim(phase, first_row, row_count, 0)
    preact = jnp.dot(samples, omega_cols, preferred_element_type=jnp.float32) + phase_cols
    return jnp.cos(preact).astype(jnp.bfloat16)


def full_gram(stacked):
    summed = gathered_total(stacked, "samp")
    return gathered_copies(summed, "tgt", 2)


def body(samples, omega, phase, right_side):
    feat_rows, col_count = right_side.shape
    samp_count = lax.axis_size("samp")
    feat_total = omega.shape[1]
    sample_total = samples.shape[0] * samp_count
    col_offset = lax.axis_index("tgt") * col_count
    store_block = math.gcd(feat_total, 512)
    stored = jnp.concatenate(
        [
            cosine_block(samples, omega, phase, index_block * store_block, store_block)
            for index_block in range(feat_total // store_block)
        ],
        axis=1,
    )

    def columns(first_row, row_count):
        return lax.dynamic_slice_in_dim(stored, first_row, row_count, 1)

    resid_all = gathered_copies(right_side, "tgt", 1)
    direction_all = resid_all
    weight_own = jnp.zeros_like(right_side)
    gram_rr = full_gram(precise_dot(resid_all.T, right_side)[None])[0]
    for iteration in range(ITERS):
        direction_own = lax.dynamic_slice_in_dim(direction_all, col_offset, col_count, 1)
        initial = jnp.zeros((samples.shape[0], col_count), jnp.float32)
        shard_piece = gathered_copies(direction_own.astype(jnp.bfloat16), "samp", 0)
        piece_rows = shard_piece.shape[0]
        block_size = math.gcd(piece_rows, 512)

        def project_one_block(index_block, acc_value):
            begin_row = index_block * block_size
            sub_piece = lax.dynamic_slice_in_dim(shard_piece, begin_row, block_size, 0)
            return acc_value + jnp.dot(
                columns(begin_row, block_size), sub_piece, preferred_element_type=jnp.float32
            )

        projected = lax.fori_loop(0, piece_rows // block_size, project_one_block, initial)
        proj_bf = projected.astype(jnp.bfloat16)
        transpose_row_count = feat_rows * lax.axis_size("samp")
        transpose_block_size = math.gcd(transpose_row_count, 512)

        def transpose_one_block(index_block, result):
            begin_row = index_block * transpose_block_size
            feats_block = columns(begin_row, transpose_block_size)
            block_term = lax.dot_general(
                feats_block, proj_bf, (((0,), (0,)), ((), ())), preferred_element_type=jnp.float32
            )
            return lax.dynamic_update_slice_in_dim(result, block_term, begin_row, 0)

        zero_rows = jnp.zeros((transpose_row_count, col_count), jnp.float32)
        summed_image = sum_at_owner(
            lax.fori_loop(
                0, transpose_row_count // transpose_block_size, transpose_one_block, zero_rows
            ),
            "samp",
            0,
        )
        image_own = summed_image / sample_total + ridge * direction_own
        image_all = gathered_copies(image_own, "tgt", 1)
        gram_pq = full_gram(precise_dot(direction_all.T, image_own)[None])[0]
        alpha_coef = spd_solve(gram_pq, gram_rr)
        alpha_own = lax.dynamic_slice_in_dim(alpha_coef, col_offset, col_count, 1)
        weight_own = weight_own + precise_dot(direction_all, alpha_own)
        if iteration + 1 < ITERS:
            resid_all = resid_all - precise_dot(image_all, alpha_coef)
            resid_now = lax.dynamic_slice_in_dim(resid_all, col_offset, col_count, 1)
            gram_new = full_gram(precise_dot(resid_all.T, resid_now)[None])[0]
            beta_coef = spd_solve(gram_rr, gram_new)
            direction_all = resid_all + precise_dot(direction_all, beta_coef)
            gram_rr = gram_new
    return weight_own


def solution(mesh):
    placed = (P("samp", None), P(), P(), P("samp", "tgt"))
    return jax.shard_map(
        body, mesh=mesh, in_specs=placed, out_specs=P("samp", "tgt"), check_vma=False
    )
```

profile of v0, /device:TPU:1, one launch (start us, length us, event | category | flops | bytes accessed | tf_op | source)
XLA Modules:
  0.0 1987.7 jit_solution(12007075214939331316)
XLA Ops:
  8.1 10.1 all-to-all-start
  21.4 2.3 fusion.21
  23.7 2.3 fusion.23
  30.4 12.1 all-to-all-start.1
  45.0 2.3 fusion.27
  47.3 2.3 fusion.29
  54.2 3.7 all-to-all-done.1
  66.4 4.1 copy.83
  70.5 2.7 reshape.132
  73.3 34.5 %all_to_all.50 = f32[64,1,4096]{2,1,0:T(1,128)} all-to-all(f32[64,1,4096]{2,1,0:T(1,128)S(1)} %reshape.132), channel_id=1, replica_groups=mesh['samp'=64,'tgt'=8] {'samp'}, dimensions={0} | all-to-all | bytes 2097152 | tf_op jit(solution)/shard_map/all_to_all | solution.py:43
  107.8 4.4 reduce.29
  119.2 8.4 all-to-all-start.5
  127.6 274.5 %all-gather.9.cloned.1.call-done = f32[32768,64]{0,1:T(8,128)} async-done(((f32[512,64]{0,1:T(8,128)}), f32[32768,64]{0,1:T(8,128)}) %all-gather.9.cloned.1.call-update) | async-done | bytes 8388624 | tf_op jit(solution)/shard_map/all_gather | solution.py:15
  402.1 8.1 copy.76
  410.2 2.4 bitcast_reduce_fusion.3
  413.8 49.6 %all-to-all-start.3 = ((f32[8,1,512,64]{2,3,1,0:T(8,128)}), f32[8,1,512,64]{2,3,1,0:T(8,128)S(1)}, u32[]{:S(2)}, u32[]{:S(2)}) async-start(f32[8,1,512,64]{2,3,1,0:T(8,128)} %broadcast_in_dim.18), calls=%async_computation.3 | async-start | bytes 2097152 | tf_op jit(solution)/shard_map/all_to_all | solution.py:27
  464.8 282.1 %all-gather.11.cloned.1.call-done = f32[32768,64]{0,1:T(8,128)} async-done(((f32[512,64]{0,1:T(8,128)}), f32[32768,64]{0,1:T(8,128)}) %all-gather.11.cloned.1.call-update) | async-done | bytes 8388624 | tf_op jit(solution)/shard_map/all_gather | solution.py:15
  746.9 8.1 copy.77
  755.0 2.4 bitcast_reduce_fusion.2
  758.8 45.4 %all-to-all-start.4 = ((f32[8,1,512,64]{2,3,1,0:T(8,128)}), f32[8,1,512,64]{2,3,1,0:T(8,128)S(1)}, u32[]{:S(2)}, u32[]{:S(2)}) async-start(f32[8,1,512,64]{2,3,1,0:T(8,128)} %broadcast_in_dim.19), calls=%async_computation.4 | async-start | bytes 2097152 | tf_op jit(solution)/shard_map/all_to_all | solution.py:27
  804.4 2.5 copy.47
  809.7 11.7 cholesky.374
  822.6 9.8 custom-call.35
  835.6 11.7 cholesky.393
  848.0 10.2 custom-call.36
  860.5 11.7 cholesky.414
  872.9 9.8 custom-call.37
  885.0 11.7 cholesky.431
  901.5 2.6 select_select_fusion.2
  904.0 11.1 while.64
  915.1 39.3 %custom-call.38 = f32[4,128,128]{1,2,0:T(8,128)S(1)} custom-call(f32[4,128,128]{2,1,0:T(8,128)S(1)} %get-tuple-element.377), custom_call_target="InvertDiagBlocksLowerTriangular" | custom-call | tf_op jit(solution)/shard_map/jit(_cho_solve)/triangular_solve | solution.py:53
  972.0 11.7 cholesky.446
  983.9 10.2 custom-call.39
  997.2 13.2 cholesky.465
  1011.8 11.3 custom-call.40
  1026.1 12.7 cholesky.486
  1039.4 10.7 custom-call.41
  1051.5 11.7 cholesky.503
  1065.1 185.6 %all-gather.13.cloned.1.call-done = f32[32768,64]{0,1:T(8,128)} async-done(((f32[512,64]{0,1:T(8,128)}), f32[32768,64]{0,1:T(8,128)}) %all-gather.13.cloned.1.call-update) | async-done | bytes 8388624 | tf_op jit(solution)/shard_map/all_gather | solution.py:15
  1250.7 8.5 copy.78
  1259.2 2.4 bitcast_reduce_fusion.1
  1262.8 47.9 %all-to-all-start.6 = ((f32[8,1,512,64]{2,3,1,0:T(8,128)}), f32[8,1,512,64]{2,3,1,0:T(8,128)}, u32[]{:S(2)}, u32[]{:S(2)}) async-start(f32[8,1,512,64]{2,3,1,0:T(8,128)} %broadcast_in_dim.21), calls=%async_computation.6 | async-start | bytes 2097152 | tf_op jit(solution)/shard_map/all_to_all | solution.py:27
  1314.2 10.9 while.65
  1325.0 39.9 %custom-call.42 = f32[4,128,128]{1,2,0:T(8,128)} custom-call(f32[4,128,128]{2,1,0:T(8,128)S(1)} %get-tuple-element.378), custom_call_target="InvertDiagBlocksLowerTriangular" | custom-call | tf_op jit(solution)/shard_map/jit(_cho_solve)/triangular_solve | solution.py:53
  1384.3 8.1 all-to-all-start.7
  1392.5 15.6 all-to-all-done.7
  1416.8 4.1 copy.82
  1420.9 2.7 reshape.138
  1423.6 34.0 %all_to_all.51 = f32[64,1,4096]{2,1,0:T(1,128)S(1)} all-to-all(f32[64,1,4096]{2,1,0:T(1,128)S(1)} %reshape.138), channel_id=1, replica_groups=mesh['samp'=64,'tgt'=8] {'samp'}, dimensions={0} | all-to-all | bytes 2097152 | tf_op jit(solution)/shard_map/all_to_all | solution.py:43
  1457.6 3.3 reduce.31
  1466.0 284.9 %all-gather.15.cloned.1.call-done = f32[32768,64]{0,1:T(8,128)} async-done(((f32[512,64]{0,1:T(8,128)}), f32[32768,64]{0,1:T(8,128)}) %all-gather.15.cloned.1.call-update) | async-done | bytes 8388624 | tf_op jit(solution)/shard_map/all_gather | solution.py:15
  1750.8 8.1 copy.79
  1759.0 2.4 bitcast_reduce_fusion
  1762.5 49.3 %all-to-all-start.9 = ((f32[8,1,512,64]{2,3,1,0:T(8,128)}), f32[8,1,512,64]{2,3,1,0:T(8,128)S(1)}, u32[]{:S(2)}, u32[]{:S(2)}) async-start(f32[8,1,512,64]{2,3,1,0:T(8,128)} %broadcast_in_dim.23), calls=%async_computation.9 | async-start | bytes 2097152 | tf_op jit(solution)/shard_map/all_to_all | solution.py:27
  1812.6 22.7 %all-to-all-done.9 = f32[8,1,512,64]{2,3,1,0:T(8,128)S(1)} async-done(((f32[8,1,512,64]{2,3,1,0:T(8,128)}), f32[8,1,512,64]{2,3,1,0:T(8,128)S(1)}, u32[]{:S(2)}, u32[]{:S(2)}) %all-to-all-start.9) | async-done | bytes 1048608 | tf_op jit(solution)/shard_map/all_to_all | solution.py:27
  1836.9 11.7 cholesky.518
  1848.8 9.8 custom-call.43
  1861.1 11.7 cholesky.537
  1872.9 10.0 custom-call.44
  1884.4 11.7 cholesky.558
  1896.2 9.8 custom-call.45
  1907.4 11.9 cholesky.575
  1924.9 8.1 while.66
  1933.0 39.3 %custom-call.46 = f32[4,128,128]{1,2,0:T(8,128)S(1)} custom-call(f32[4,128,128]{2,1,0:T(8,128)S(1)} %get-tuple-element.379), custom_call_target="InvertDiagBlocksLowerTriangular" | custom-call | tf_op jit(solution)/shard_map/jit(_cho_solve)/triangular_solve | solution.py:53
  (298 shorter events, 173.0 us)
Async XLA Ops:
  6.5 12.5 copy-start
  8.1 18.5 all-to-all-start
  30.4 27.5 %all-to-all-start.1 = ((bf16[64,2,2048]{2,1,0:T(2,128)(2,1)}), bf16[64,2,2048]{2,1,0:T(2,128)(2,1)}, u32[]{:S(2)}, u32[]{:S(2)}) async-start(bf16[64,2,2048]{2,1,0:T(2,128)(2,1)} %reshape.130), calls=%async_computation.1 | async-start | bytes 1048576 | tf_op jit(solution)/shard_map/all_to_all | solution.py:27
  42.5 359.6 %all-gather.9.cloned.1.call-start = ((), (), s32[]{:S(2)}) async-start(), calls=%async_computation.10 | async-start | bytes 8519680 | tf_op jit(solution)/shard_map/all_gather | solution.py:15
  114.3 3.0 copy-start.20
  117.3 629.6 %all-gather.11.cloned.1.call-start = ((), (), s32[]{:S(2)}) async-start(), calls=%async_computation.11 | async-start | bytes 8519680 | tf_op jit(solution)/shard_map/all_gather | solution.py:15
  119.2 293.4 %all-to-all-start.5 = ((f32[8,1,4096]{2,1,0:T(1,128)}), f32[8,1,4096]{2,1,0:T(1,128)S(1)}, u32[]{:S(2)}, u32[]{:S(2)}) async-start(f32[8,1,4096]{2,1,0:T(1,128)} %reshape.134), calls=%async_computation.5 | async-start | bytes 262144 | tf_op jit(solution)/shard_map/all_to_all | solution.py:27
  413.8 343.6 %all-to-all-start.3 = ((f32[8,1,512,64]{2,3,1,0:T(8,128)}), f32[8,1,512,64]{2,3,1,0:T(8,128)S(1)}, u32[]{:S(2)}, u32[]{:S(2)}) async-start(f32[8,1,512,64]{2,3,1,0:T(8,128)} %broadcast_in_dim.18), calls=%async_computation.3 | async-start | bytes 2097152 | tf_op jit(solution)/shard_map/all_to_all | solution.py:27
  757.4 1.4 copy-start.2
  758.8 195.7 %all-to-all-start.4 = ((f32[8,1,512,64]{2,3,1,0:T(8,128)}), f32[8,1,512,64]{2,3,1,0:T(8,128)S(1)}, u32[]{:S(2)}, u32[]{:S(2)}) async-start(f32[8,1,512,64]{2,3,1,0:T(8,128)} %broadcast_in_dim.19), calls=%async_computation.4 | async-start | bytes 2097152 | tf_op jit(solution)/shard_map/all_to_all | solution.py:27
  804.2 446.5 %all-gather.13.cloned.1.call-start = ((), (), s32[]{:S(2)}) async-start(), calls=%async_computation.12 | async-start | bytes 8519680 | tf_op jit(solution)/shard_map/all_gather | solution.py:15
  808.7 1.0 copy-start.5
  954.5 5.2 copy-start.16
  954.5 2.3 copy-start.4
  960.1 3.4 copy-start.17
  963.9 2.5 copy-start.13
  964.9 0.7 copy-start.18
  966.4 0.7 copy-start.21
  970.9 1.1 copy-start.6
  1262.8 102.2 %all-to-all-start.6 = ((f32[8,1,512,64]{2,3,1,0:T(8,128)}), f32[8,1,512,64]{2,3,1,0:T(8,128)}, u32[]{:S(2)}, u32[]{:S(2)}) async-start(f32[8,1,512,64]{2,3,1,0:T(8,128)} %broadcast_in_dim.21), calls=%async_computation.6 | async-start | bytes 2097152 | tf_op jit(solution)/shard_map/all_to_all | solution.py:27
  1365.0 9.0 copy-start.3
  1372.5 4.1 copy-start.11
  1372.5 4.6 copy-start.15
  1374.0 3.5 copy-start.9
  1380.2 1.4 copy-start.22
  1384.3 23.8 %all-to-all-start.7 = ((bf16[64,2,2048]{2,1,0:T(2,128)(2,1)}), bf16[64,2,2048]{2,1,0:T(2,128)(2,1)}, u32[]{:S(2)}, u32[]{:S(2)}) async-start(bf16[64,2,2048]{2,1,0:T(2,128)(2,1)} %reshape.136), calls=%async_computation.7 | async-start | bytes 1048576 | tf_op jit(solution)/shard_map/all_to_all | solution.py:27
  1392.5 358.4 %all-gather.15.cloned.1.call-start = ((), (), s32[]{:S(2)}) async-start(), calls=%async_computation.13 | async-start | bytes 8519680 | tf_op jit(solution)/shard_map/all_gather | solution.py:15
  1761.4 50.5 %copy-start.14 = (f32[128,512]{1,0:T(8,128)S(1)}, f32[128,512]{1,0:T(8,128)}, u32[]{:S(2)}) copy-start(f32[128,512]{1,0:T(8,128)} %copy-done.13) | copy-start | bytes 786436
  1761.4 50.5 %copy-start.19 = (f32[128,512]{1,0:T(8,128)S(1)}, f32[128,512]{1,0:T(8,128)}, u32[]{:S(2)}) copy-start(f32[128,512]{1,0:T(8,128)} %copy-done.18) | copy-start | bytes 786436
  1762.5 72.8 %all-to-all-start.9 = ((f32[8,1,512,64]{2,3,1,0:T(8,128)}), f32[8,1,512,64]{2,3,1,0:T(8,128)S(1)}, u32[]{:S(2)}, u32[]{:S(2)}) async-start(f32[8,1,512,64]{2,3,1,0:T(8,128)} %broadcast_in_dim.23), calls=%async_computation.9 | async-start | bytes 2097152 | tf_op jit(solution)/shard_map/all_to_all | solution.py:27
  1835.9 1.0 copy-start.7
  1924.7 49.0 %copy-start.8 = (f32[128,512]{1,0:T(8,128)S(1)}, f32[128,512]{1,0:T(8,128)}, u32[]{:S(2)}) copy-start(f32[128,512]{1,0:T(8,128)} %copy.73) | copy-start | bytes 786436
  1924.8 49.7 %copy-start.12 = (f32[128,512]{1,0:T(8,128)S(1)}, f32[128,512]{1,0:T(8,128)}, u32[]{:S(2)}) copy-start(f32[128,512]{1,0:T(8,128)} %copy.74) | copy-start | bytes 786436
  1973.7 1.7 copy-start.10
  1978.1 2.8 copy-start.1
Sparse Core Ops, SparseCore 0:
  117.4 284.5 all-gather.8
  404.1 342.6 all-gather.10
  968.2 282.4 all-gather.12
  1466.1 284.6 all-gather.14
where the time goes:
time: 2000 us; the launch traced here: 1990 us
  waiting for transfers between devices  1070 us (54%)
  other arithmetic  394 us (20%)
  starting transfers between devices  231 us (12%)
  local copies, waits for them, and re-layouts  123 us (6%)
  matrix products  78.2 us (4%)
  blocking collectives  68.6 us (3%)
  between operations  21.8 us (1%)
    all_gather x4, waiting for transfers between devices, gathered_total(): tiles = lax.all_gather(value, axis)  1030 us
    another operation x43, other arithmetic, spd_solve(): factor = jnp.linalg.cholesky(gram_matrix)  245 us
    all_to_all x8, starting transfers between devices, sent_to_all(): lax.all_to_all(jnp.broadcast_to(value[None], (length, *value.shape)), axi...  231 us
    another operation x8, other arithmetic, spd_solve(): return jax.scipy.linalg.cho_solve((factor, True), rhs_matrix)  122 us
    all_to_all x2, blocking collectives, sum_at_owner(): lax.all_to_all(tiles, axis, split_axis=0, concat_axis=0, tiled=True)  68.6 us
    unnamed x65, local copies, waits for them, and re-layouts  62.2 us
    all_to_all x8, waiting for transfers between devices, sent_to_all(): lax.all_to_all(jnp.broadcast_to(value[None], (length, *value.shape)), axi...  42.7 us
  transfers between devices with their start and end apart: 12, of which 8 were waited for; matrix products, arithmetic and copies ran while one was open for 17% of the time, Pallas kernels for 0%

commit v1 on v0

v1 whole, which is shorter than its diff:
```python
import jax
import jax.numpy as jnp
from jax import lax
from jax.experimental import pallas as pl
from jax.experimental.pallas import tpu as pltpu
from jax.sharding import PartitionSpec as P

f32 = jnp.float32
bf16 = jnp.bfloat16
MESH = pl.DeviceIdType.MESH
VMEM = pl.BlockSpec(memory_space=pltpu.VMEM)
RIDGE = 1.0

NX, NZ, NY, NU, NC = 4, 8, 2, 4, 2
COLS = 64
PAIR = 128
SLOTS = NX * NZ
CHUNK = 24
GRAM = CHUNK * NZ
TOTAL = NU * NC * COLS
BK = 128
PN = 8
NT = (((1,), (1,)), ((), ()))
NN = (((1,), (0,)), ((), ()))


def fine(a, b, dims=NN):
    return lax.dot_general(a, b, dims, precision=lax.Precision.HIGHEST, preferred_element_type=f32)


def quick(a, b, dims=NN):
    return lax.dot_general(a, b, dims, preferred_element_type=f32)


class Place:
    def __init__(self, send_sem, recv_sem):
        samp, tgt = lax.axis_index("samp"), lax.axis_index("tgt")
        self.x, self.z, self.y = samp // 16, (samp % 16) // 2, samp % 2
        self.u, self.c = tgt // 2, tgt % 2
        self.slot = self.x * NZ + self.z
        self.send_sem, self.recv_sem, self.used = send_sem, recv_sem, 0

    def at(self, x=None, z=None, y=None, u=None, c=None):
        x, z, y = (own if new is None else new for own, new in ((self.x, x), (self.z, z), (self.y, y)))
        u, c = (own if new is None else new for own, new in ((self.u, u), (self.c, c)))
        return (x * 16 + z * 2 + y, u * 2 + c)

    def z_peers(self):
        return [lax.rem(self.z + d, NZ) for d in range(1, NZ)]

    def x_peers(self):
        return [lax.rem(self.x + d, NX) for d in range(1, NX)]

    def u_peers(self):
        return [lax.rem(self.u + d, NU) for d in range(1, NU)]

    def xy_peers(self):
        return [(lax.rem(self.x + d, NX), y) for d in range(NX) for y in (self.y, 1 - self.y)][1:]

    def greet(self):
        devices = [self.at(z=z) for z in self.z_peers()]
        devices += [self.at(x=x, y=y) for x, y in self.xy_peers()]
        devices += [self.at(u=u) for u in self.u_peers()] + [self.at(c=1 - self.c)]
        barrier = pltpu.get_barrier_semaphore()
        for device in devices:
            pl.semaphore_signal(barrier, inc=1, device_id=device, device_id_type=MESH)
        pl.semaphore_wait(barrier, len(devices))

    def send(self, src, dst, device):
        index = self.used
        self.used += 1
        copy = pltpu.make_async_remote_copy(
            src_ref=src,
            dst_ref=dst,
            send_sem=self.send_sem.at[index],
            recv_sem=self.recv_sem.at[index],
            device_id=device,
            device_id_type=MESH,
        )
        copy.start()
        return copy


def finish(copies):
    for copy in copies:
        copy.wait()


def run(*works):
    works = list(works)
    while works:
        works = [work for work in works if next(work, "end") != "end"]


def gather_slots(here, block, parts):
    rest = block
    for part in parts:
        part[here.slot] = rest.astype(bf16)
        rest = rest - rest.astype(bf16).astype(f32)
    along_z = [[here.send(p.at[here.slot], p.at[here.slot], here.at(z=z)) for z in here.z_peers()] for p in parts]
    yield
    along_x = []
    for p, copies in zip(parts, along_z):
        finish(copies)
        own = p.at[pl.ds(here.x * NZ, NZ)]
        along_x.append([here.send(own, own, here.at(x=x)) for x in here.x_peers()])
    for copies in along_x:
        yield
        finish(copies)


def gather_targets(here, ref):
    own = ref.at[here.u, here.c]
    copies = [here.send(own, own, here.at(u=u)) for u in here.u_peers()]
    yield
    finish(copies)
    own = ref.at[:, here.c]
    copies = [here.send(own, own, here.at(c=1 - here.c))]
    yield
    finish(copies)


def gram_sum(here, part, out, from_z, from_xy):
    copies = [
        here.send(part.at[pl.ds(z * CHUNK, CHUNK)], from_z.at[i], here.at(z=z)) for i, z in enumerate(here.z_peers())
    ]
    yield
    finish(copies)
    rows = pl.ds(pl.multiple_of(here.z * CHUNK, CHUNK), CHUNK)
    total = part[rows]
    for i in range(NZ - 1):
        total = total + from_z[i]
    index = here.x * NY + here.y
    from_xy[index] = total
    copies = [here.send(from_xy.at[index], from_xy.at[index], here.at(x=x, y=y)) for x, y in here.xy_peers()]
    yield
    finish(copies)
    total = from_xy[0]
    for i in range(1, NX * NY):
        total = total + from_xy[i]
    out[here.u, here.c, rows] = total
    own = out.at[here.u, here.c, rows]
    copies = [here.send(own, own, here.at(u=u)) for u in here.u_peers()]
    yield
    finish(copies)
    own = out.at[:, here.c, rows]
    copies = [here.send(own, own, here.at(z=z)) for z in here.z_peers()]
    yield
    finish(copies)
    own = out.at[:, here.c]
    copies = [here.send(own, own, here.at(c=1 - here.c))]
    yield
    finish(copies)


def gram_share(here, left, right):
    mask = lax.broadcasted_iota(jnp.int32, (COLS, PAIR), 1) // COLS == here.y
    whole = right[here.u].reshape(NC * COLS, PAIR)
    shares = []
    for d in range(3):
        rows = left[lax.rem(here.u + d, NU), here.c]
        shares.append(fine(jnp.where(mask, rows, 0.0), whole, NT))
    return jnp.concatenate(shares, axis=0)


def project(slots, feats, ref):
    samples = feats.shape[0]
    ref[...] = jnp.zeros_like(ref)

    def one(i, carry):
        at = pl.ds(pl.multiple_of(i * PAIR, PAIR), PAIR)
        return carry + quick(slots[i], feats[:, at], NT)

    total = lax.fori_loop(0, SLOTS, one, jnp.zeros((COLS, samples), f32))
    ref[:, :samples] = total


def first_kernel(
    total_samples, feats, block, b_all, q_all, t_all, gram_s, gram_m,
    from_y, high, low, proj, proj_low, t_err, share_s, share_m, sz, sxy, mz, mxy, image, image_x, image_z, sum_x, sum_z, image_y,
    send_sem, recv_sem,
):
    here = Place(send_sem, recv_sem)
    samples = feats.shape[0]
    here.greet()
    copy = here.send(block, from_y, here.at(y=1 - here.y))
    copy.wait()
    b_all[here.u, here.c] = block[...] + from_y[...]

    def gram_of_start():
        yield from gather_targets(here, b_all)
        share_m[...] = gram_share(here, b_all, b_all)
        yield from gram_sum(here, share_m, gram_m, mz, mxy)

    sum_of_start = gram_of_start()
    gathering = gather_slots(here, b_all[here.u, here.c], (high, low))
    next(sum_of_start)
    next(gathering)
    next(gathering)
    next(sum_of_start)
    next(gathering)
    project(high, feats, proj)
    t_all[here.u, here.c] = proj[...].astype(bf16)
    targets_t = gather_targets(here, t_all)
    next(targets_t)
    next(sum_of_start)

    rounded = proj[:, :samples].astype(bf16)

    def one(i, carry):
        at = pl.ds(pl.multiple_of(i * PAIR, PAIR), PAIR)
        image[i] = quick(rounded, feats[:, at]).astype(bf16)
        return carry

    lax.fori_loop(0, SLOTS, one, 0)

    def sum_of_image():
        copies = [
            here.send(image.at[pl.ds(x * NZ, NZ)], image_x.at[i], here.at(x=x)) for i, x in enumerate(here.x_peers())
        ]
        yield
        finish(copies)
        total = image[pl.ds(here.x * NZ, NZ)].astype(f32)
        for i in range(NX - 1):
            total = total + image_x[i].astype(f32)
        sum_x[...] = total
        copies = [here.send(sum_x.at[z], image_z.at[i], here.at(z=z)) for i, z in enumerate(here.z_peers())]
        yield
        finish(copies)
        total = sum_x[here.z]
        for i in range(NZ - 1):
            total = total + image_z[i]
        sum_z[...] = total
        copies = [here.send(sum_z, image_y, here.at(y=1 - here.y))]
        yield
        finish(copies)
        total = sum_z[...] + image_y[...]
        q_all[here.u, here.c] = total * (1.0 / total_samples) + RIDGE * b_all[here.u, here.c]
        yield from gather_targets(here, q_all)

    def gram_of_image():
        yield from gathering
        project(low, feats, proj_low)
        t_err[here.u, here.c] = (proj[...] - proj[...].astype(bf16).astype(f32) + proj_low[...]).astype(bf16)
        targets_e = gather_targets(here, t_err)
        next(targets_e)
        next(targets_t)
        yield
        yield from targets_e
        next(targets_t, None)
        right = t_all[here.u].reshape(NC * COLS, -1)
        right_err = t_err[here.u].reshape(NC * COLS, -1)
        shares = []
        for d in range(3):
            at = lax.rem(here.u + d, NU)
            value, err = t_all[at, here.c], t_err[at, here.c]
            cross = quick(err, right, NT) + quick(value, right_err, NT)
            shares.append(quick(value, right, NT) + 0.5 * cross)
        gram = jnp.concatenate(shares, axis=0) * (1.0 / total_samples)
        share_s[...] = gram + RIDGE * share_m[...]
        yield from gram_sum(here, share_s, gram_s, sz, sxy)

    run(gram_of_image(), sum_of_image(), sum_of_start)


def second_kernel(feats, r_all, v_all, gram_r, high, proj, share, rz, rxy, send_sem, recv_sem):
    here = Place(send_sem, recv_sem)
    here.greet()
    share[...] = gram_share(here, r_all, r_all)

    def targets():
        yield from gather_slots(here, r_all[here.u, here.c], (high,))
        project(high, feats, proj)
        v_all[here.u, here.c] = proj[...].astype(bf16)
        yield from gather_targets(here, v_all)

    run(gram_sum(here, share, gram_r, rz, rxy), targets())


def third_kernel(share, gram_p, pz, pxy, send_sem, recv_sem):
    here = Place(send_sem, recv_sem)
    here.greet()
    run(gram_sum(here, share, gram_p, pz, pxy))


def invert_blocks(blocks):
    count = BK // PN
    row = lax.broadcasted_iota(jnp.int32, (PN, BK), 0)
    lane = lax.broadcasted_iota(jnp.int32, (PN, BK), 1)
    mats = [[b[g * PN : (g + 1) * PN, :] for g in range(count)] for b in blocks]

    def wide(v, j):
        return jnp.broadcast_to(v[:, j : j + 1], (PN, BK))

    def tall(v, i):
        return jnp.broadcast_to(v[i : i + 1, :], (PN, BK))

    for p in range(count):
        base = p * PN
        inside = (lane >= base) & (lane < base + PN)
        reduced = []
        for m in mats:
            panel = m[p]
            cols = [wide(panel, base + k) for k in range(PN)]
            for i in range(PN):
                inv = 1.0 / tall(cols[i], i)
                here = row == i
                factor = jnp.where(here, 0.0, cols[i])
                src = jnp.where(lane == base + i, jnp.where(here, 1.0, 0.0), panel)
                pivot = tall(src, i) * inv
                panel = jnp.where(here, pivot, src - factor * pivot)
                for k in range(i + 1, PN):
                    top = tall(cols[k], i) * inv
                    cols[k] = jnp.where(here, top, cols[k] - factor * top)
            reduced.append(panel)
        for m, panel in zip(mats, reduced):
            rows = [tall(panel, k) for k in range(PN)]
            for g in [(p + 1 + g) % count for g in range(count - 1)]:
                acc = jnp.where(inside, 0.0, m[g])
                for k in range(PN):
                    acc = acc - wide(m[g], base + k) * rows[k]
                m[g] = acc
            m[p] = panel
    return [jnp.concatenate(m, axis=0) for m in mats]


def invert(refs):
    steps = TOTAL // BK
    eye = jnp.where(
        lax.broadcasted_iota(jnp.int32, (BK, BK), 0) == lax.broadcasted_iota(jnp.int32, (BK, BK), 1), 1.0, 0.0
    )

    def one(k, carry):
        at = pl.ds(pl.multiple_of(k * BK, BK), BK)
        inverses = invert_blocks([ref[at, at] for ref in refs])
        for ref, inverse in zip(refs, inverses):
            ref[at, at] = eye
            head = fine(inverse, ref[at, :])
            for d in range(1, steps):
                i = lax.rem(k + d, steps)
                ai = pl.ds(pl.multiple_of(i * BK, BK), BK)
                left = ref[ai, at]
                ref[ai, at] = jnp.zeros((BK, BK), f32)
                ref[ai, :] = ref[ai, :] - fine(left, head)
            ref[at, :] = head
        return carry

    lax.fori_loop(0, steps, one, 0)


def assemble(gram, ref):
    for u in range(NU):
        for d in range(3):
            r = (u + d) % NU
            block = gram[u, :, d * COLS : (d + 1) * COLS, :].reshape(BK, BK)
            ref[r * BK : (r + 1) * BK, u * BK : (u + 1) * BK] = block
            if d == 1:
                ref[u * BK : (u + 1) * BK, r * BK : (r + 1) * BK] = block.T


def alpha_kernel(gram_s, gram_m, b_all, q_all, m_inv, alpha_t, r_all, s_inv, m_full):
    assemble(gram_s, s_inv)
    assemble(gram_m, m_full)
    m_inv[...] = m_full[...]
    invert([s_inv, m_inv])
    alpha_t[...] = fine(m_full[...], s_inv[...])
    r_all[...] = b_all[...] - fine(alpha_t[...], q_all[...])


def beta_kernel(total_samples, gram_r, m_inv, r_all, b_all, v_all, t_all, p_all, r_full, share, t1, beta_t):
    tgt = lax.axis_index("tgt")
    y = lax.axis_index("samp") % 2
    u, c = tgt // 2, tgt % 2
    assemble(gram_r, r_full)
    beta_t[...] = fine(r_full[...], m_inv[...])
    p_all[...] = r_all[...] + fine(beta_t[...], b_all[...])
    t1[...] = (v_all[...].astype(f32) + fine(beta_t[...], t_all[...].astype(f32))).astype(bf16)
    mask = lax.broadcasted_iota(jnp.int32, (COLS, PAIR), 1) // COLS == y
    own = pl.ds(pl.multiple_of(u * 2 * COLS, 2 * COLS), 2 * COLS)
    right_p, right_t = p_all[own, :], t1[own, :]
    for d in range(3):
        at = pl.ds(pl.multiple_of((lax.rem(u + d, NU) * 2 + c) * COLS, COLS), COLS)
        gram = quick(t1[at, :], right_t, NT) * (1.0 / total_samples)
        share[d * COLS : (d + 1) * COLS, :] = gram + RIDGE * fine(jnp.where(mask, p_all[at, :], 0.0), right_p, NT)


def weight_kernel(gram_p, r_full, alpha_t, b_all, p_all, out, p_inv):
    tgt = lax.axis_index("tgt")
    y = lax.axis_index("samp") % 2
    own = pl.ds(pl.multiple_of(tgt * COLS, COLS), COLS)
    assemble(gram_p, p_inv)
    invert([p_inv])
    last_t = fine(r_full[own, :], p_inv[...])
    weights = fine(alpha_t[own, :], b_all[...]) + fine(last_t, p_all[...])
    mine = jnp.where(y == 0, weights[:, :COLS], weights[:, COLS:])
    out[...] = mine.T


def shape(dims, dtype=f32):
    return jax.ShapeDtypeStruct(dims, dtype)


def call(kernel, name, args, outs, scratch, collective_id=None):
    params = dict(vmem_limit_bytes=60 * 2**20)
    if collective_id is not None:
        params.update(collective_id=collective_id, has_side_effects=True)
    return pl.pallas_call(
        kernel,
        out_shape=outs,
        in_specs=[VMEM] * len(args),
        out_specs=[VMEM] * len(outs),
        scratch_shapes=scratch,
        name=name,
        compiler_params=pltpu.CompilerParams(**params),
    )(*args)


def copies(count):
    return [pltpu.SemaphoreType.DMA((count,))] * 2


def body(samples, omega, phase, right_side):
    count = samples.shape[0]
    lanes = 2 * PAIR
    total_samples = count * lax.axis_size("samp")
    y = lax.axis_index("samp") % 2
    preact = jnp.dot(samples, omega, preferred_element_type=f32) + phase
    feats = jnp.cos(preact).astype(bf16)
    turned = right_side.T
    zero = jnp.zeros_like(turned)
    block = jnp.concatenate([jnp.where(y == 0, turned, zero), jnp.where(y == 1, turned, zero)], axis=1)

    vm = pltpu.VMEM
    all_feats = (NU, NC, COLS, PAIR)
    all_samples = (NU, NC, COLS, lanes)
    gram = (NU, NC, GRAM, BK)
    sums = [vm((NZ - 1, CHUNK, BK), f32), vm((NX * NY, CHUNK, BK), f32)]
    slots = vm((SLOTS, COLS, PAIR), bf16)
    b_all, q_all, t_all, gram_s, gram_m = call(
        lambda *refs: first_kernel(total_samples, *refs),
        "first",
        (feats, block),
        [shape(all_feats), shape(all_feats), shape(all_samples, bf16), shape(gram), shape(gram)],
        [
            vm((COLS, PAIR), f32), slots, slots, vm((COLS, lanes), f32), vm((COLS, lanes), f32), vm(all_samples, bf16),
            vm((GRAM, BK), f32), vm((GRAM, BK), f32), *sums, *sums,
            slots, vm((NX - 1, NZ, COLS, PAIR), bf16), vm((NZ - 1, COLS, PAIR), f32),
            vm((NZ, COLS, PAIR), f32), vm((COLS, PAIR), f32), vm((COLS, PAIR), f32),
        ]
        + copies(104),
        1,
    )
    flat = (TOTAL, PAIR)
    full = (TOTAL, TOTAL)
    b_flat = b_all.reshape(flat)
    m_inv, alpha_t, r_all = call(
        alpha_kernel,
        "alpha",
        (gram_s, gram_m, b_flat, q_all.reshape(flat)),
        [shape(full), shape(full), shape(flat)],
        [vm(full, f32), vm(full, f32)],
    )
    v_all, gram_r = call(
        second_kernel,
        "second",
        (feats, r_all.reshape(all_feats)),
        [shape(all_samples, bf16), shape(gram)],
        [slots, vm((COLS, lanes), f32), vm((GRAM, BK), f32), *sums] + copies(48),
        2,
    )
    p_all, r_full, share = call(
        lambda *refs: beta_kernel(total_samples, *refs),
        "beta",
        (gram_r, m_inv, r_all, b_flat, v_all.reshape(TOTAL, lanes), t_all.reshape(TOTAL, lanes)),
        [shape(flat), shape(full), shape((GRAM, BK))],
        [vm((TOTAL, lanes), bf16), vm(full, f32)],
    )
    (gram_p,) = call(third_kernel, "third", (share,), [shape(gram)], sums + copies(32), 3)
    (out,) = call(
        weight_kernel, "weight", (gram_p, r_full, alpha_t, b_flat, p_all), [shape((COLS, COLS))], [vm(full, f32)]
    )
    return out


def solution(mesh):
    placed = (P("samp", None), P(), P(), P("samp", "tgt"))
    return jax.shard_map(body, mesh=mesh, in_specs=placed, out_specs=P("samp", "tgt"), check_vma=False)
```

time: 2000 us -> 264 us (0.13)
  waiting for transfers between devices: 1070 us -> 0 us
  other arithmetic: 394 us -> 0.71 us
  Pallas kernels: 0 us -> 249 us
  starting transfers between devices: 231 us -> 0 us
  local copies, waits for them, and re-layouts: 123 us -> 0.92 us
  blocking collectives: 68.6 us -> 0 us
  matrix products: 78.2 us -> 12.8 us
  between operations: 21.8 us -> 0.04 us
    all_gather x4 -> x0, waiting for transfers between devices: 1030 us -> none  [gathered_total(): tiles = lax.all_gather(value, axis)]
    another operation x51 -> x0, other arithmetic: 368 us -> none  [the longest x43 245 us: spd_solve(): factor = jnp.linalg.cholesky(gram_matrix)]
    pallas_call x0 -> x6, Pallas kernels: none -> 249 us  [call(): pl.pallas_call(kernel, out_shape=outs, in_specs=[VMEM] * len(args), out_s...]
    all_to_all x8 -> x0, starting transfers between devices: 231 us -> none  [sent_to_all(): lax.all_to_all(jnp.broadcast_to(value[None], (length, *value.shape)), axi...]
    all_to_all x2 -> x0, blocking collectives: 68.6 us -> none  [sum_at_owner(): lax.all_to_all(tiles, axis, split_axis=0, concat_axis=0, tiled=True)]
    unnamed x65 -> x3, local copies, waits for them, and re-layouts: 62.2 us -> 0.92 us
    another operation x60 -> x0, matrix products: 45.9 us -> none  [the longest x42 26.3 us: spd_solve(): return jax.scipy.linalg.cho_solve((factor, True), rhs_matrix)]
    all_to_all x8 -> x0, waiting for transfers between devices: 42.7 us -> none  [sent_to_all(): lax.all_to_all(jnp.broadcast_to(value[None], (length, *value.shape)), axi...]
  transfers between devices with their start and end apart: 12 -> 0, of which waited for: 8 -> 0; matrix products, arithmetic and copies ran while one was open for 17% -> 0% of each run, Pallas kernels for 0% -> 0%
where the time goes in v1:
time: 264 us
  Pallas kernels  249 us (94%)
  matrix products  12.8 us (5%)
    pallas_call x6, Pallas kernels, call(): pl.pallas_call(kernel, out_shape=outs, in_specs=[VMEM] * len(args), out_s...  249 us
    dot_general x1, matrix products, body(): preact = jnp.dot(samples, omega, preferred_element_type=f32) + phase  12.8 us

profile of v1, /device:TPU:1, one launch (start us, length us, event | category | flops | bytes accessed | tf_op | source)
XLA Modules:
  0.0 263.8 jit_solution(15180573623798969700)
XLA Ops:
  0.0 0.0 copy-start
  0.0 0.9 copy.5
  0.9 0.7 pad_maximum_fusion.refs_1_
  1.6 0.0 copy-done
  1.6 12.8 %fusion.1.refs_0_.feats = bf16[192,4096]{1,0:T(8,128)(2,1)} fusion(bf16[192,128]{1,0:T(8,128)(2,1)} %param.4, bf16[128,4096]{1,0:T(8,128)(2,1)S(1)} %copy-done, f32[4096]{0:T(1024)} %param.6), kind=kOutput, calls=%fused_computation.2 | convolution fusion | flops 202899456 | bytes 2686976 | tf_op jit(solution)/shard_map/dot_general | solution.py:427
  14.5 94.4 %first.1 = (f32[4,2,64,128]{3,2,1,0:T(8,128)}, f32[4,2,64,128]{3,2,1,0:T(8,128)}, bf16[4,2,64,256]{3,2,1,0:T(8,128)(2,1)}, f32[4,2,192,128]{3,2,1,0:T(8,128)}, f32[4,2,192,128]{3,2,1,0:T(8,128)}) custom-call(bf16[192,4096]{1,0:T(8,128)(2,1)} %fusion.1.refs_0_.feats, f32[64,128]{1,0:T(8,128)} %pad_maximum_fusion.refs_1_), custom_call_target="tpu_custom_call" | custom-call | tf_op jit(solution)/shard_map/first/pallas_call | solution.py:407
  108.9 46.8 %alpha.1 = (f32[512,512]{1,0:T(8,128)}, f32[512,512]{1,0:T(8,128)}, f32[512,128]{1,0:T(8,128)}) custom-call(f32[4,2,192,128]{3,2,1,0:T(8,128)} %get-tuple-element.18.gram_s, f32[4,2,192,128]{3,2,1,0:T(8,128)} %get-tuple-element.19.gram_m, f32[512,128]{1,0:T(8,128)} %bitcast.11, f32[512,128]{1,0:T(8,128)} %bitcast.17), custom_call_target="tpu_custom_call" | custom-call | tf_op jit(solution)/shard_map/alpha/pallas_call | solution.py:407
  155.8 42.3 %second.1 = (bf16[4,2,64,256]{3,2,1,0:T(8,128)(2,1)}, f32[4,2,192,128]{3,2,1,0:T(8,128)}) custom-call(bf16[192,4096]{1,0:T(8,128)(2,1)} %fusion.1.refs_0_.feats, f32[4,2,64,128]{3,2,1,0:T(8,128)} %bitcast.14), custom_call_target="tpu_custom_call" | custom-call | tf_op jit(solution)/shard_map/second/pallas_call | solution.py:407
  198.0 7.7 %beta.1 = (f32[512,128]{1,0:T(8,128)}, f32[512,512]{1,0:T(8,128)}, f32[192,128]{1,0:T(8,128)}) custom-call(f32[4,2,192,128]{3,2,1,0:T(8,128)} %get-tuple-element.23.refs_0_, f32[512,512]{1,0:T(8,128)} %get-tuple-element.24.refs_1_, f32[512,128]{1,0:T(8,128)} %get-tuple-element.22.refs_2_, f32[512,128]{1,0:T(8,128)} %bitcast.12, bf16[512,256]{1,0:T(8,128)(2,1)} %bitcast.16, ...), custom_call_target="tpu_custom_call" | custom-call | tf_op jit(solution)/shard_map/beta/pallas_call | solution.py:407
  205.7 31.7 %third.1.gram_p = f32[4,2,192,128]{3,2,1,0:T(8,128)} custom-call(f32[192,128]{1,0:T(8,128)} %get-tuple-element.27.share), custom_call_target="tpu_custom_call" | custom-call | tf_op jit(solution)/shard_map/third/pallas_call | solution.py:407
  237.5 26.4 %weight.1 = f32[64,64]{1,0:T(8,128)} custom-call(f32[4,2,192,128]{3,2,1,0:T(8,128)} %third.1.gram_p, f32[512,512]{1,0:T(8,128)} %get-tuple-element.28.r_full, f32[512,512]{1,0:T(8,128)} %get-tuple-element.29.alpha_t, f32[512,128]{1,0:T(8,128)} %bitcast.13, f32[512,128]{1,0:T(8,128)} %get-tuple-element.30.p_all), custom_call_target="tpu_custom_call" | custom-call | tf_op jit(solution)/shard_map/weight/pallas_call | solution.py:407
  (1 shorter events, 0.0 us)
Async XLA Ops:
  0.0 1.6 copy-start

commit v2 on v0

v2 whole, which is shorter than its diff:
```python
import jax
import jax.numpy as jnp
from jax import lax
from jax.experimental import pallas as pl
from jax.experimental.pallas import tpu as pltpu
from jax.sharding import PartitionSpec as P

f32 = jnp.float32
bf16 = jnp.bfloat16
MESH = pl.DeviceIdType.MESH
VMEM = pl.BlockSpec(memory_space=pltpu.VMEM)
RIDGE = 1.0

NX, NZ, NY, NU, NC = 4, 8, 2, 4, 2
COLS = 64
PAIR = 128
SLOTS = NX * NZ
CHUNK = 24
GRAM = CHUNK * NZ
TOTAL = NU * NC * COLS
BK = 128
PN = 8
COPIES = 200
NT = (((1,), (1,)), ((), ()))
NN = (((1,), (0,)), ((), ()))


def fine(a, b, dims=NN):
    return lax.dot_general(a, b, dims, precision=lax.Precision.HIGHEST, preferred_element_type=f32)


def quick(a, b, dims=NN):
    return lax.dot_general(a, b, dims, preferred_element_type=f32)


class Place:
    def __init__(self, send_sem, recv_sem):
        samp, tgt = lax.axis_index("samp"), lax.axis_index("tgt")
        self.x, self.z, self.y = samp // 16, (samp % 16) // 2, samp % 2
        self.u, self.c = tgt // 2, tgt % 2
        self.slot = self.x * NZ + self.z
        self.send_sem, self.recv_sem, self.used = send_sem, recv_sem, 0

    def at(self, x=None, z=None, y=None, u=None, c=None):
        x, z, y = (own if new is None else new for own, new in ((self.x, x), (self.z, z), (self.y, y)))
        u, c = (own if new is None else new for own, new in ((self.u, u), (self.c, c)))
        return (x * 16 + z * 2 + y, u * 2 + c)

    def z_peers(self):
        return [lax.rem(self.z + d, NZ) for d in range(1, NZ)]

    def x_peers(self):
        return [lax.rem(self.x + d, NX) for d in range(1, NX)]

    def u_peers(self):
        return [lax.rem(self.u + d, NU) for d in range(1, NU)]

    def xy_peers(self):
        return [(lax.rem(self.x + d, NX), y) for d in range(NX) for y in (self.y, 1 - self.y)][1:]

    def greet(self):
        devices = [self.at(z=z) for z in self.z_peers()]
        devices += [self.at(x=x, y=y) for x, y in self.xy_peers()]
        devices += [self.at(u=u) for u in self.u_peers()] + [self.at(c=1 - self.c)]
        barrier = pltpu.get_barrier_semaphore()
        for device in devices:
            pl.semaphore_signal(barrier, inc=1, device_id=device, device_id_type=MESH)
        self.greeted = len(devices)

    def meet(self):
        pl.semaphore_wait(pltpu.get_barrier_semaphore(), self.greeted)

    def step(self, make):
        return Step(self, make)


class Step:
    def __init__(self, here, make):
        self.here, self.make = here, make
        self.first = here.used
        here.used += len(make())

    def copies(self):
        return [
            pltpu.make_async_remote_copy(
                src_ref=src,
                dst_ref=dst,
                send_sem=self.here.send_sem.at[self.first + i],
                recv_sem=self.here.recv_sem.at[self.first + i],
                device_id=device,
                device_id_type=MESH,
            )
            for i, (src, dst, device) in enumerate(self.make())
        ]

    def start(self):
        for copy in self.copies():
            copy.start()

    def wait(self):
        for copy in self.copies():
            copy.wait()


def run(*works):
    works = list(works)
    while works:
        works = [work for work in works if next(work, "end") != "end"]


def gather_slots(here, part):
    along_z = here.step(
        lambda: [(part.at[here.slot], part.at[here.slot], here.at(z=z)) for z in here.z_peers()]
    )
    along_z.start()
    yield
    along_z.wait()

    def to_x():
        own = part.at[pl.ds(here.x * NZ, NZ)]
        return [(own, own, here.at(x=x)) for x in here.x_peers()]

    along_x = here.step(to_x)
    along_x.start()
    yield
    along_x.wait()


def gather_near(here, ref):
    def near():
        own = ref.at[here.u, here.c]
        return [(own, own, here.at(u=u)) for u in here.u_peers()] + [(own, own, here.at(c=1 - here.c))]

    step = here.step(near)
    step.start()
    yield
    step.wait()


def swap_rest(here, ref):
    def rest():
        copies = []
        for u in here.u_peers():
            block = ref.at[u, here.c]
            copies.append((block, block, here.at(c=1 - here.c)))
        return copies

    step = here.step(rest)
    step.start()
    yield
    step.wait()


def gather_targets(here, ref):
    yield from gather_near(here, ref)
    yield from swap_rest(here, ref)


def gram_sum(here, part, out, from_z, from_xy):
    spread = here.step(
        lambda: [
            (part.at[pl.ds(z * CHUNK, CHUNK)], from_z.at[i], here.at(z=z)) for i, z in enumerate(here.z_peers())
        ]
    )
    spread.start()
    yield
    spread.wait()
    total = part[pl.ds(pl.multiple_of(here.z * CHUNK, 8), CHUNK)]
    for i in range(NZ - 1):
        total = total + from_z[i]
    from_xy[here.x * NY + here.y] = total

    def to_xy():
        own = from_xy.at[here.x * NY + here.y]
        return [(own, own, here.at(x=x, y=y)) for x, y in here.xy_peers()]

    across = here.step(to_xy)
    across.start()
    yield
    across.wait()
    total = from_xy[0]
    for i in range(1, NX * NY):
        total = total + from_xy[i]
    out[here.u, here.c, pl.ds(pl.multiple_of(here.z * CHUNK, 8), CHUNK)] = total

    def to_u():
        own = out.at[here.u, here.c, pl.ds(here.z * CHUNK, CHUNK)]
        return [(own, own, here.at(u=u)) for u in here.u_peers()]

    along_u = here.step(to_u)
    along_u.start()
    yield
    along_u.wait()

    def to_z():
        own = out.at[:, here.c, pl.ds(here.z * CHUNK, CHUNK)]
        return [(own, own, here.at(z=z)) for z in here.z_peers()]

    along_z = here.step(to_z)
    along_z.start()
    yield
    along_z.wait()
    swap = here.step(lambda: [(out.at[:, here.c], out.at[:, here.c], here.at(c=1 - here.c))])
    swap.start()
    yield
    swap.wait()


def gram_share(here, left, right):
    mask = lax.broadcasted_iota(jnp.int32, (COLS, PAIR), 1) // COLS == here.y
    whole = right[here.u].reshape(NC * COLS, PAIR)
    shares = []
    for d in range(3):
        rows = left[lax.rem(here.u + d, NU), here.c]
        shares.append(fine(jnp.where(mask, rows, 0.0), whole, NT))
    return jnp.concatenate(shares, axis=0)


def project(slots, feats, first, count):
    def group(i, total):
        index = lax.rem(first + i, NX)
        for z in range(NZ):
            at = pl.ds(pl.multiple_of((index * NZ + z) * PAIR, PAIR), PAIR)
            total = total + quick(slots[index * NZ + z], feats[:, at], NT)
        return total

    return lax.fori_loop(0, count, group, jnp.zeros((COLS, feats.shape[0]), f32))


def cosine(x):
    n = jnp.floor(x * 0.3183098861837907 + 0.5)
    r = ((x - n * 3.140625) - n * 0.0009670257568359375) - n * 6.2771141529083251953e-07
    half = n * 0.5
    sign = 1.0 - 4.0 * (half - jnp.floor(half))
    q = r * r
    poly = 1.0 / 479001600.0
    for term in (-1.0 / 3628800.0, 1.0 / 40320.0, -1.0 / 720.0, 1.0 / 24.0, -0.5, 1.0):
        poly = poly * q + term
    return sign * poly


def invert_blocks(blocks):
    count = BK // PN
    row = lax.broadcasted_iota(jnp.int32, (PN, BK), 0)
    lane = lax.broadcasted_iota(jnp.int32, (PN, BK), 1)
    mats = [[b[g * PN : (g + 1) * PN, :] for g in range(count)] for b in blocks]

    def wide(v, j):
        return jnp.broadcast_to(v[:, j : j + 1], (PN, BK))

    def tall(v, i):
        return jnp.broadcast_to(v[i : i + 1, :], (PN, BK))

    for p in range(count):
        base = p * PN
        inside = (lane >= base) & (lane < base + PN)
        reduced = []
        for m in mats:
            panel = m[p]
            cols = [wide(panel, base + k) for k in range(PN)]
            for i in range(PN):
                inv = 1.0 / tall(cols[i], i)
                here = row == i
                factor = jnp.where(here, 0.0, cols[i])
                src = jnp.where(lane == base + i, jnp.where(here, 1.0, 0.0), panel)
                pivot = tall(src, i) * inv
                panel = jnp.where(here, pivot, src - factor * pivot)
                for k in range(i + 1, PN):
                    top = tall(cols[k], i) * inv
                    cols[k] = jnp.where(here, top, cols[k] - factor * top)
            reduced.append(panel)
        for m, panel in zip(mats, reduced):
            rows = [tall(panel, k) for k in range(PN)]
            for g in [(p + 1 + g) % count for g in range(count - 1)]:
                acc = jnp.where(inside, 0.0, m[g])
                for k in range(PN):
                    acc = acc - wide(m[g], base + k) * rows[k]
                m[g] = acc
            m[p] = panel
    return [jnp.concatenate(m, axis=0) for m in mats]


def reduce_block(ref, k, at, hook):
    (inverse,) = invert_blocks([ref[at, at]])
    ref[at, at] = inverse
    hook()
    inverse = ref[at, at]
    rows = lax.broadcasted_iota(jnp.int32, (TOTAL, BK), 0)
    cols = lax.broadcasted_iota(jnp.int32, (BK, BK), 1)
    ref[at, at] = jnp.where(lax.broadcasted_iota(jnp.int32, (BK, BK), 0) == cols, 1.0, 0.0)
    head = fine(inverse, ref[at, :])
    left = jnp.where(rows // BK == k, 0.0, ref[:, at])
    ref[:, at] = jnp.zeros((TOTAL, BK), f32)
    ref[...] = ref[...] - fine(left, head)
    ref[at, :] = head


def invert(ref, hooks=None):
    steps = TOTAL // BK
    if hooks is None:

        def one(k, carry):
            reduce_block(ref, k, pl.ds(pl.multiple_of(k * BK, BK), BK), lambda: None)
            return carry

        lax.fori_loop(0, steps, one, 0)
    else:
        for k in range(steps):
            reduce_block(ref, k, pl.ds(k * BK, BK), hooks[2 * k])
            hooks[2 * k + 1]()


def assemble(gram, ref):
    for u in range(NU):
        for d in range(3):
            r = (u + d) % NU
            block = gram[u, :, d * COLS : (d + 1) * COLS, :].reshape(BK, BK)
            ref[r * BK : (r + 1) * BK, u * BK : (u + 1) * BK] = block
            if d == 1:
                ref[u * BK : (u + 1) * BK, r * BK : (r + 1) * BK] = block.T


def later(*works):
    def hook():
        for work in works:
            next(work, None)

    return hook


def kernel(
    total_samples, samples, omega, phase, right_side, out,
    feats, block, from_y, b_all, q_all, r_all, t_all, t_err, v_all, high, low, high_r, proj, image, image_x, image_z, sum_x,
    sum_z, image_y, share_m, share_s, share_r, share_p, gram_sm, gram_r, gram_p, mz, mxy, sz, sxy, rz, rxy,
    pz, pxy, inv_sm, p_inv, m_high, m_low, m_full, r_full, alpha_t, beta_t, p_all, t1, send_sem, recv_sem,
):
    here = Place(send_sem, recv_sem)
    count, lanes = samples.shape[0], t_all.shape[-1]
    flat = (TOTAL, PAIR)
    here.greet()
    mine = lax.broadcasted_iota(jnp.int32, (COLS, PAIR), 1) // COLS == here.y
    turned = right_side[...].T
    block[...] = jnp.where(mine, jnp.concatenate([turned, turned], axis=1), 0.0)

    def features(first, chunks):
        width = 2 * PAIR

        def one(i, carry):
            at = pl.ds(pl.multiple_of((first + i) * width, width), width)
            feats[:, at] = cosine(quick(samples[...], omega[:, at]) + phase[:, at]).astype(bf16)
            return carry

        lax.fori_loop(0, chunks, one, 0)

    scope = jax.named_scope
    gram_s, gram_m = gram_sm.at[0], gram_sm.at[1]
    s_inv, m_inv = inv_sm.at[0], inv_sm.at[1]
    with scope("feat1"):
        features(0, 8)
    with scope("meet"):
        here.meet()
    pair = here.step(lambda: [(block, from_y, here.at(y=1 - here.y))])
    pair.start()
    with scope("feat2"):
        features(8, 4)
        t_all[...] = jnp.zeros_like(t_all)
        t_err[...] = jnp.zeros_like(t_err)
        v_all[...] = jnp.zeros_like(v_all)
    with scope("pairwait"):
        pair.wait()
        both = block[...] + from_y[...]
        b_all[here.u, here.c] = both
        high[here.slot] = both.astype(bf16)
        low[here.slot] = (both - both.astype(bf16).astype(f32)).astype(bf16)
    gather_high, gather_low = gather_slots(here, high), gather_slots(here, low)
    targets_b = gather_near(here, b_all)
    next(gather_high)
    next(targets_b)
    next(gather_low)
    with scope("feat3"):
        features(12, 4)
    with scope("waithz"):
        next(gather_high)
    with scope("proj1"):
        proj[...] = project(high, feats, here.x, 1)
    with scope("waitlz"):
        next(gather_low)
    with scope("waitb"):
        next(targets_b, None)
    rest_b = swap_rest(here, b_all)
    with scope("sharem"):
        share_m[...] = gram_share(here, b_all, b_all)
    sum_m = gram_sum(here, share_m, gram_m, mz, mxy)
    next(sum_m)
    next(rest_b)
    with scope("waithx"):
        next(gather_high, None)
    with scope("proj2"):
        proj[...] = proj[...] + project(high, feats, here.x + 1, NX - 1)
        t_all[here.u, here.c, :, :count] = proj[...].astype(bf16)
    targets_t = gather_near(here, t_all)
    next(targets_t)
    with scope("m_z"):
        next(sum_m)

    with scope("image"):
        rounded = proj[...].astype(bf16)

        def image_group(i, carry):
            for z in range(NZ):
                at = pl.ds(pl.multiple_of((i * NZ + z) * PAIR, PAIR), PAIR)
                image[i * NZ + z] = quick(rounded, feats[:, at]).astype(bf16)
            return carry

        lax.fori_loop(0, NX, image_group, 0)

    def sum_of_image():
        def to_x():
            return [
                (image.at[pl.ds(x * NZ, NZ)], image_x.at[i], here.at(x=x)) for i, x in enumerate(here.x_peers())
            ]

        along_x = here.step(to_x)
        along_x.start()
        yield
        along_x.wait()
        total = image[pl.ds(here.x * NZ, NZ)].astype(f32)
        for i in range(NX - 1):
            total = total + image_x[i].astype(f32)
        sum_x[...] = total
        along_z = here.step(
            lambda: [(sum_x.at[z], image_z.at[i], here.at(z=z)) for i, z in enumerate(here.z_peers())]
        )
        along_z.start()
        yield
        along_z.wait()
        total = sum_x[here.z]
        for i in range(NZ - 1):
            total = total + image_z[i]
        sum_z[...] = total
        along_y = here.step(lambda: [(sum_z, image_y, here.at(y=1 - here.y))])
        along_y.start()
        yield
        along_y.wait()
        total = sum_z[...] + image_y[...]
        q_all[here.u, here.c] = total * (1.0 / total_samples) + RIDGE * b_all[here.u, here.c]
        yield from gather_targets(here, q_all)

    with scope("m_xy"):
        next(sum_m)
    with scope("waitlx"):
        next(gather_low, None)
    with scope("proj3"):
        exact = proj[...] + project(low, feats, 0, NX)
        t_err[here.u, here.c, :, :count] = (exact - proj[...].astype(bf16).astype(f32)).astype(bf16)
    targets_e = gather_near(here, t_err)
    next(targets_e)
    image_sum = sum_of_image()
    next(image_sum)
    with scope("m_u"):
        next(sum_m)
    with scope("waitt"):
        next(targets_t, None)
    with scope("waite"):
        next(targets_e, None)
    with scope("shares"):
        right = t_all[here.u].reshape(NC * COLS, lanes)
        right_err = t_err[here.u].reshape(NC * COLS, lanes)
        for d in range(3):
            at = lax.rem(here.u + d, NU)
            value, err = t_all[at, here.c], t_err[at, here.c]
            cross = quick(err, right, NT) + quick(value, right_err, NT)
            rows = pl.ds(d * COLS, COLS)
            share_s[rows] = (quick(value, right, NT) + 0.5 * cross) * (1.0 / total_samples) + RIDGE * share_m[rows]
    sum_s = gram_sum(here, share_s, gram_s, sz, sxy)
    next(sum_s)
    rest_t = swap_rest(here, t_all)
    next(rest_t)
    with scope("s_z"):
        next(sum_s)
    with scope("s_xy"):
        next(sum_s)
    with scope("m_z2"):
        next(sum_m)
    with scope("s_u"):
        next(sum_s)
    with scope("m_end"):
        next(sum_m, None)
    with scope("s_z2"):
        next(sum_s)
    with scope("s_end"):
        next(sum_s, None)

    mine_inv = inv_sm.at[here.c]
    with scope("assemble"):
        assemble(gram_sm.at[here.c], mine_inv)
    side, idle = later(image_sum), later()
    with scope("inverse1"):
        invert(mine_inv, [side, idle, side, side, idle, side, side, idle])
    swap = here.step(lambda: [(inv_sm.at[here.c], inv_sm.at[here.c], here.at(c=1 - here.c))])
    swap.start()
    with scope("drain"):
        run(rest_b, rest_t, image_sum)
        assemble(gram_m, m_full)
    with scope("swap"):
        swap.wait()
    with scope("alpha"):
        alpha_t[...] = fine(m_full[...], s_inv[...])
    with scope("resid"):
        residual = b_all[...].reshape(flat) - fine(alpha_t[...], q_all[...].reshape(flat))
        r_all[...] = residual.reshape(r_all.shape)
        high_r[here.slot] = r_all[here.u, here.c].astype(bf16)
    gather_r = gather_slots(here, high_r)
    next(gather_r)
    with scope("sharer"):
        share_r[...] = gram_share(here, r_all, r_all)
    sum_r = gram_sum(here, share_r, gram_r, rz, rxy)
    next(sum_r)
    with scope("m_split"):
        m_high[...] = m_inv[...].astype(bf16)
        m_low[...] = (m_inv[...] - m_high[...].astype(f32)).astype(bf16)
    with scope("r_gz"):
        next(gather_r)
    with scope("r_z"):
        next(sum_r)
    with scope("r_xy"):
        next(sum_r)
    with scope("r_gx"):
        next(gather_r, None)
    with scope("proj4"):
        v_all[here.u, here.c, :, :count] = project(high_r, feats, 0, NX).astype(bf16)
    gather_v = gather_targets(here, v_all)
    next(gather_v)
    with scope("r_u"):
        next(sum_r)
    with scope("v_u"):
        next(gather_v)
    with scope("r_z2"):
        next(sum_r)
    with scope("r_end"):
        run(sum_r, gather_v)

    with scope("beta"):
        assemble(gram_r, r_full)
        upper = r_full[...].astype(bf16)
        lower = (r_full[...] - upper.astype(f32)).astype(bf16)
        beta_t[...] = quick(upper, m_high[...]) + (quick(lower, m_high[...]) + quick(upper, m_low[...]))
    with scope("pdir"):
        p_all[...] = r_all[...].reshape(flat) + fine(beta_t[...], b_all[...].reshape(flat))
    with scope("tdir"):
        t_flat = t_all[...].reshape(TOTAL, lanes)
        upper = beta_t[...].astype(bf16)
        lower = (beta_t[...] - upper.astype(f32)).astype(bf16)
        moved = quick(upper, t_flat) + quick(lower, t_flat)
        t1[...] = (v_all[...].reshape(TOTAL, lanes).astype(f32) + moved).astype(bf16)
    with scope("sharep"):
        own = pl.ds(pl.multiple_of(here.u * 2 * COLS, 2 * COLS), 2 * COLS)
        right_p, right_t = p_all[own, :], t1[own, :]
        for d in range(3):
            at = pl.ds(pl.multiple_of((lax.rem(here.u + d, NU) * 2 + here.c) * COLS, COLS), COLS)
            gram = quick(t1[at, :], right_t, NT) * (1.0 / total_samples)
            share_p[pl.ds(d * COLS, COLS)] = gram + RIDGE * fine(jnp.where(mine, p_all[at, :], 0.0), right_p, NT)
    with scope("sump"):
        sum_p = gram_sum(here, share_p, gram_p, pz, pxy)
        next(sum_p)
        own = pl.ds(pl.multiple_of((here.u * 2 + here.c) * COLS, COLS), COLS)
        weights = fine(alpha_t[own, :], b_all[...].reshape(flat))
        run(sum_p)
    with scope("inverse2"):
        assemble(gram_p, p_inv)
        invert(p_inv)
    with scope("final"):
        last_t = fine(r_full[own, :], p_inv[...])
        weights = weights + fine(last_t, p_all[...])
        out[...] = jnp.where(here.y == 0, weights[:, :COLS], weights[:, COLS:]).T


def body(samples, omega, phase, right_side):
    count = samples.shape[0]
    total_samples = count * lax.axis_size("samp")
    vm = pltpu.VMEM
    all_feats = vm((NU, NC, COLS, PAIR), f32)
    all_samples = vm((NU, NC, COLS, 2 * PAIR), bf16)
    share = vm((GRAM, BK), f32)
    gram = vm((NU, NC, GRAM, BK), f32)
    sums = [vm((NZ - 1, CHUNK, BK), f32), vm((NX * NY, CHUNK, BK), f32)]
    slots = vm((SLOTS, COLS, PAIR), bf16)
    block = vm((COLS, PAIR), f32)
    full, half = vm((TOTAL, TOTAL), f32), vm((TOTAL, TOTAL), bf16)
    grams, fulls = vm((2, NU, NC, GRAM, BK), f32), vm((2, TOTAL, TOTAL), f32)
    scratch = [vm((count, omega.shape[1]), bf16), block, block, all_feats, all_feats, all_feats]
    scratch += [all_samples, all_samples, all_samples, slots, slots, slots, vm((COLS, count), f32)]
    scratch += [slots, vm((NX - 1, NZ, COLS, PAIR), bf16), vm((NZ - 1, COLS, PAIR), f32), vm((NZ, COLS, PAIR), f32)]
    scratch += [block, block, share, share, share, share, grams, gram, gram, *sums, *sums, *sums, *sums]
    scratch += [fulls, full, half, half, full, full, full, full, vm((TOTAL, PAIR), f32), vm((TOTAL, 2 * PAIR), bf16)]
    scratch += [pltpu.SemaphoreType.DMA((COPIES,))] * 2
    return pl.pallas_call(
        lambda *refs: kernel(total_samples, *refs),
        out_shape=jax.ShapeDtypeStruct(right_side.shape, f32),
        in_specs=[VMEM] * 4,
        out_specs=VMEM,
        scratch_shapes=scratch,
        name="cg",
        compiler_params=pltpu.CompilerParams(vmem_limit_bytes=60 * 2**20, collective_id=1, has_side_effects=True),
    )(samples, omega, phase.reshape(1, -1), right_side)


def solution(mesh):
    placed = (P("samp", None), P(), P(), P("samp", "tgt"))
    return jax.shard_map(body, mesh=mesh, in_specs=placed, out_specs=P("samp", "tgt"), check_vma=False)
```

time: 2000 us -> 201 us (0.10)
  waiting for transfers between devices: 1070 us -> 0 us
  other arithmetic: 394 us -> 0 us
  starting transfers between devices: 231 us -> 0 us
  Pallas kernels: 0 us -> 199 us
  local copies, waits for them, and re-layouts: 123 us -> 1.38 us
  matrix products: 78.2 us -> 0 us
  blocking collectives: 68.6 us -> 0 us
  between operations: 21.8 us -> 0.01 us
    all_gather x4 -> x0, waiting for transfers between devices: 1030 us -> none  [gathered_total(): tiles = lax.all_gather(value, axis)]
    another operation x51 -> x0, other arithmetic: 368 us -> none  [the longest x43 245 us: spd_solve(): factor = jnp.linalg.cholesky(gram_matrix)]
    all_to_all x8 -> x0, starting transfers between devices: 231 us -> none  [sent_to_all(): lax.all_to_all(jnp.broadcast_to(value[None], (length, *value.shape)), axi...]
    pallas_call x0 -> x1, Pallas kernels: none -> 199 us  [body(): pl.pallas_call(lambda *refs: kernel(total_samples, *refs), out_shape=jax....]
    all_to_all x2 -> x0, blocking collectives: 68.6 us -> none  [sum_at_owner(): lax.all_to_all(tiles, axis, split_axis=0, concat_axis=0, tiled=True)]
    unnamed x65 -> x1, local copies, waits for them, and re-layouts: 62.2 us -> 1.38 us
    another operation x60 -> x0, matrix products: 45.9 us -> none  [the longest x42 26.3 us: spd_solve(): return jax.scipy.linalg.cho_solve((factor, True), rhs_matrix)]
    all_to_all x8 -> x0, waiting for transfers between devices: 42.7 us -> none  [sent_to_all(): lax.all_to_all(jnp.broadcast_to(value[None], (length, *value.shape)), axi...]
  transfers between devices with their start and end apart: 12 -> 0, of which waited for: 8 -> 0; matrix products, arithmetic and copies ran while one was open for 17% -> 0% of each run, Pallas kernels for 0% -> 0%
where the time goes in v2:
time: 201 us
  Pallas kernels  199 us (99%)
    pallas_call x1, Pallas kernels, body(): pl.pallas_call(lambda *refs: kernel(total_samples, *refs), out_shape=jax....  199 us

profile of v2, /device:TPU:1, one launch (start us, length us, event | category | flops | bytes accessed | tf_op | source)
XLA Modules:
  0.0 200.7 jit_solution(13587730292819422854)
XLA Ops:
  0.0 199.3 %cg.1 = f32[64,64]{1,0:T(8,128)} custom-call(bf16[192,128]{1,0:T(8,128)(2,1)} %refs_0_.1, bf16[128,4096]{1,0:T(8,128)(2,1)} %refs_1_.1, f32[1,4096]{1,0:T(1,128)} %bitcast.1, f32[64,64]{1,0:T(8,128)} %refs_3_.1), custom_call_target="tpu_custom_call" | custom-call | tf_op jit(solution)/shard_map/cg/pallas_call | solution.py:597
  199.3 1.4 copy.6

commit v3 on v2

--- a/solution.py
+++ b/solution.py
@@ -16,7 +16,7 @@
 PAIR = 128
 SLOTS = NX * NZ
 CHUNK = 24
-GRAM = CHUNK * NZ
+GRAM = CHUNK * NX * NY
 TOTAL = NU * NC * COLS
 BK = 128
 PN = 8
@@ -126,10 +126,10 @@
     along_x.wait()
 
 
-def gather_near(here, ref):
+def gather_near(here, ref, skip=0):
     def near():
         own = ref.at[here.u, here.c]
-        return [(own, own, here.at(u=u)) for u in here.u_peers()] + [(own, own, here.at(c=1 - here.c))]
+        return [(own, own, here.at(u=u)) for u in here.u_peers()[skip:]] + [(own, own, here.at(c=1 - here.c))]
 
     step = here.step(near)
     step.start()
@@ -156,50 +156,48 @@
     yield from swap_rest(here, ref)
 
 
-def gram_sum(here, part, out, from_z, from_xy):
+def gram_sum(here, part, out, from_xy, from_z):
+    def chunk(x, y):
+        return pl.ds(pl.multiple_of((x * NY + y) * CHUNK, 8), CHUNK)
+
     spread = here.step(
         lambda: [
-            (part.at[pl.ds(z * CHUNK, CHUNK)], from_z.at[i], here.at(z=z)) for i, z in enumerate(here.z_peers())
+            (part.at[chunk(x, y)], from_xy.at[i], here.at(x=x, y=y)) for i, (x, y) in enumerate(here.xy_peers())
         ]
     )
     spread.start()
     yield
     spread.wait()
-    total = part[pl.ds(pl.multiple_of(here.z * CHUNK, 8), CHUNK)]
-    for i in range(NZ - 1):
+    total = part[chunk(here.x, here.y)]
+    for i in range(NX * NY - 1):
+        total = total + from_xy[i]
+    from_z[here.z] = total
+    along_z = here.step(lambda: [(from_z.at[here.z], from_z.at[here.z], here.at(z=z)) for z in here.z_peers()])
+    along_z.start()
+    yield
+    along_z.wait()
+    total = from_z[0]
+    for i in range(1, NZ):
         total = total + from_z[i]
-    from_xy[here.x * NY + here.y] = total
+    out[here.u, here.c, chunk(here.x, here.y)] = total
+
+    def to_u():
+        own = out.at[here.u, here.c, chunk(here.x, here.y)]
+        return [(own, own, here.at(u=u)) for u in here.u_peers()]
+
+    along_u = here.step(to_u)
+    along_u.start()
+    yield
+    along_u.wait()
 
     def to_xy():
-        own = from_xy.at[here.x * NY + here.y]
+        own = out.at[:, here.c, chunk(here.x, here.y)]
         return [(own, own, here.at(x=x, y=y)) for x, y in here.xy_peers()]
 
     across = here.step(to_xy)
     across.start()
     yield
     across.wait()
-    total = from_xy[0]
-    for i in range(1, NX * NY):
-        total = total + from_xy[i]
-    out[here.u, here.c, pl.ds(pl.multiple_of(here.z * CHUNK, 8), CHUNK)] = total
-
-    def to_u():
-        own = out.at[here.u, here.c, pl.ds(here.z * CHUNK, CHUNK)]
-        return [(own, own, here.at(u=u)) for u in here.u_peers()]
-
-    along_u = here.step(to_u)
-    along_u.start()
-    yield
-    along_u.wait()
-
-    def to_z():
-        own = out.at[:, here.c, pl.ds(here.z * CHUNK, CHUNK)]
-        return [(own, own, here.at(z=z)) for z in here.z_peers()]
-
-    along_z = here.step(to_z)
-    along_z.start()
-    yield
-    along_z.wait()
     swap = here.step(lambda: [(out.at[:, here.c], out.at[:, here.c], here.at(c=1 - here.c))])
     swap.start()
     yield
@@ -330,9 +328,9 @@
 
 def kernel(
     total_samples, samples, omega, phase, right_side, out,
-    feats, block, from_y, b_all, q_all, r_all, t_all, t_err, v_all, high, low, high_r, proj, image, image_x, image_z, sum_x,
-    sum_z, image_y, share_m, share_s, share_r, share_p, gram_sm, gram_r, gram_p, mz, mxy, sz, sxy, rz, rxy,
-    pz, pxy, inv_sm, p_inv, m_high, m_low, m_full, r_full, alpha_t, beta_t, p_all, t1, send_sem, recv_sem,
+    feats, block, from_y, b_all, q_all, r_all, t_all, t_err, v_all, high, low, high_r, proj, proj_low, image, image_x, image_z, sum_x,
+    sum_z, image_y, share_m, share_s, share_r, share_p, gram_sm, gram_r, gram_p, mxy, mz, sxy, sz, rxy, rz,
+    pxy, pz, inv_sm, p_inv, m_high, m_low, m_full, r_full, alpha_t, beta_t, p_all, t1, send_sem, recv_sem,
 ):
     here = Place(send_sem, recv_sem)
     count, lanes = samples.shape[0], t_all.shape[-1]
@@ -379,20 +377,23 @@
     next(gather_low)
     with scope("feat3"):
         features(12, 4)
-    with scope("waithz"):
-        next(gather_high)
-    with scope("proj1"):
-        proj[...] = project(high, feats, here.x, 1)
-    with scope("waitlz"):
-        next(gather_low)
     with scope("waitb"):
         next(targets_b, None)
     rest_b = swap_rest(here, b_all)
     with scope("sharem"):
         share_m[...] = gram_share(here, b_all, b_all)
-    sum_m = gram_sum(here, share_m, gram_m, mz, mxy)
+    sum_m = gram_sum(here, share_m, gram_m, mxy, mz)
     next(sum_m)
     next(rest_b)
+    with scope("waithz"):
+        next(gather_high)
+    with scope("waitlz"):
+        next(gather_low)
+    with scope("proj1"):
+        proj[...] = project(high, feats, here.x, 1)
+        proj_low[...] = project(low, feats, here.x, 1)
+    with scope("m_xy"):
+        next(sum_m)
     with scope("waithx"):
         next(gather_high, None)
     with scope("proj2"):
@@ -400,8 +401,6 @@
         t_all[here.u, here.c, :, :count] = proj[...].astype(bf16)
     targets_t = gather_near(here, t_all)
     next(targets_t)
-    with scope("m_z"):
-        next(sum_m)
 
     with scope("image"):
         rounded = proj[...].astype(bf16)
@@ -446,17 +445,16 @@
         q_all[here.u, here.c] = total * (1.0 / total_samples) + RIDGE * b_all[here.u, here.c]
         yield from gather_targets(here, q_all)
 
-    with scope("m_xy"):
+    with scope("m_z"):
         next(sum_m)
     with scope("waitlx"):
         next(gather_low, None)
     with scope("proj3"):
-        exact = proj[...] + project(low, feats, 0, NX)
+        exact = proj[...] + (proj_low[...] + project(low, feats, here.x + 1, NX - 1))
         t_err[here.u, here.c, :, :count] = (exact - proj[...].astype(bf16).astype(f32)).astype(bf16)
-    targets_e = gather_near(here, t_err)
+    targets_e = gather_near(here, t_err, 1)
     next(targets_e)
     image_sum = sum_of_image()
-    next(image_sum)
     with scope("m_u"):
         next(sum_m)
     with scope("waitt"):
@@ -472,21 +470,24 @@
             cross = quick(err, right, NT) + quick(value, right_err, NT)
             rows = pl.ds(d * COLS, COLS)
             share_s[rows] = (quick(value, right, NT) + 0.5 * cross) * (1.0 / total_samples) + RIDGE * share_m[rows]
-    sum_s = gram_sum(here, share_s, gram_s, sz, sxy)
+    sum_s = gram_sum(here, share_s, gram_s, sxy, sz)
     next(sum_s)
+    next(image_sum)
     rest_t = swap_rest(here, t_all)
     next(rest_t)
+    with scope("s_xy"):
+        next(sum_s)
+    with scope("m_xy2"):
+        next(sum_m)
     with scope("s_z"):
         next(sum_s)
-    with scope("s_xy"):
-        next(sum_s)
-    with scope("m_z2"):
-        next(sum_m)
+    with scope("image_x"):
+        next(image_sum)
     with scope("s_u"):
         next(sum_s)
     with scope("m_end"):
         next(sum_m, None)
-    with scope("s_z2"):
+    with scope("s_xy2"):
         next(sum_s)
     with scope("s_end"):
         next(sum_s, None)
@@ -496,7 +497,7 @@
         assemble(gram_sm.at[here.c], mine_inv)
     side, idle = later(image_sum), later()
     with scope("inverse1"):
-        invert(mine_inv, [side, idle, side, side, idle, side, side, idle])
+        invert(mine_inv, [side, idle, side, idle, side, idle, side, idle])
     swap = here.step(lambda: [(inv_sm.at[here.c], inv_sm.at[here.c], here.at(c=1 - here.c))])
     swap.start()
     with scope("drain"):
@@ -514,28 +515,31 @@
     next(gather_r)
     with scope("sharer"):
         share_r[...] = gram_share(here, r_all, r_all)
-    sum_r = gram_sum(here, share_r, gram_r, rz, rxy)
+    sum_r = gram_sum(here, share_r, gram_r, rxy, rz)
     next(sum_r)
     with scope("m_split"):
         m_high[...] = m_inv[...].astype(bf16)
         m_low[...] = (m_inv[...] - m_high[...].astype(f32)).astype(bf16)
+    with scope("r_xy"):
+        next(sum_r)
     with scope("r_gz"):
         next(gather_r)
+    with scope("proj3"):
+        proj[...] = project(high_r, feats, here.x, 1)
     with scope("r_z"):
-        next(sum_r)
-    with scope("r_xy"):
         next(sum_r)
     with scope("r_gx"):
         next(gather_r, None)
     with scope("proj4"):
-        v_all[here.u, here.c, :, :count] = project(high_r, feats, 0, NX).astype(bf16)
+        v_own = proj[...] + project(high_r, feats, here.x + 1, NX - 1)
+        v_all[here.u, here.c, :, :count] = v_own.astype(bf16)
     gather_v = gather_targets(here, v_all)
     next(gather_v)
     with scope("r_u"):
         next(sum_r)
     with scope("v_u"):
         next(gather_v)
-    with scope("r_z2"):
+    with scope("r_xy2"):
         next(sum_r)
     with scope("r_end"):
         run(sum_r, gather_v)
@@ -561,7 +565,7 @@
             gram = quick(t1[at, :], right_t, NT) * (1.0 / total_samples)
             share_p[pl.ds(d * COLS, COLS)] = gram + RIDGE * fine(jnp.where(mine, p_all[at, :], 0.0), right_p, NT)
     with scope("sump"):
-        sum_p = gram_sum(here, share_p, gram_p, pz, pxy)
+        sum_p = gram_sum(here, share_p, gram_p, pxy, pz)
         next(sum_p)
         own = pl.ds(pl.multiple_of((here.u * 2 + here.c) * COLS, COLS), COLS)
         weights = fine(alpha_t[own, :], b_all[...].reshape(flat))
@@ -583,13 +587,13 @@
     all_samples = vm((NU, NC, COLS, 2 * PAIR), bf16)
     share = vm((GRAM, BK), f32)
     gram = vm((NU, NC, GRAM, BK), f32)
-    sums = [vm((NZ - 1, CHUNK, BK), f32), vm((NX * NY, CHUNK, BK), f32)]
+    sums = [vm((NX * NY - 1, CHUNK, BK), f32), vm((NZ, CHUNK, BK), f32)]
     slots = vm((SLOTS, COLS, PAIR), bf16)
     block = vm((COLS, PAIR), f32)
     full, half = vm((TOTAL, TOTAL), f32), vm((TOTAL, TOTAL), bf16)
     grams, fulls = vm((2, NU, NC, GRAM, BK), f32), vm((2, TOTAL, TOTAL), f32)
     scratch = [vm((count, omega.shape[1]), bf16), block, block, all_feats, all_feats, all_feats]
-    scratch += [all_samples, all_samples, all_samples, slots, slots, slots, vm((COLS, count), f32)]
+    scratch += [all_samples, all_samples, all_samples, slots, slots, slots, vm((COLS, count), f32), vm((COLS, count), f32)]
     scratch += [slots, vm((NX - 1, NZ, COLS, PAIR), bf16), vm((NZ - 1, COLS, PAIR), f32), vm((NZ, COLS, PAIR), f32)]
     scratch += [block, block, share, share, share, share, grams, gram, gram, *sums, *sums, *sums, *sums]
     scratch += [fulls, full, half, half, full, full, full, full, vm((TOTAL, PAIR), f32), vm((TOTAL, 2 * PAIR), bf16)]

time: 201 us -> 176 us (0.88)
  Pallas kernels: 199 us -> 174 us
    pallas_call x1, Pallas kernels: 199 us -> 174 us  [body(): pl.pallas_call(lambda *refs: kernel(total_samples, *refs), out_shape=jax....]
where the time goes in v3:
time: 176 us
  Pallas kernels  174 us (99%)
    pallas_call x1, Pallas kernels, body(): pl.pallas_call(lambda *refs: kernel(total_samples, *refs), out_shape=jax....  174 us

profile of v3, /device:TPU:1, one launch (start us, length us, event | category | flops | bytes accessed | tf_op | source)
XLA Modules:
  0.0 175.8 jit_solution(12092895054847789020)
XLA Ops:
  0.0 174.5 %cg.1 = f32[64,64]{1,0:T(8,128)} custom-call(bf16[192,128]{1,0:T(8,128)(2,1)} %refs_0_.1, bf16[128,4096]{1,0:T(8,128)(2,1)} %refs_1_.1, f32[1,4096]{1,0:T(1,128)} %bitcast.1, f32[64,64]{1,0:T(8,128)} %refs_3_.1), custom_call_target="tpu_custom_call" | custom-call | tf_op jit(solution)/shard_map/cg/pallas_call | solution.py:601
  174.5 1.4 copy.6

commit v4 on v3

--- a/solution.py
+++ b/solution.py
@@ -20,7 +20,8 @@
 TOTAL = NU * NC * COLS
 BK = 128
 PN = 8
-COPIES = 200
+COPIES = 340
+NEAREST = (0, 1, 7, 2, 6, 3, 5, 4)
 NT = (((1,), (1,)), ((), ()))
 NN = (((1,), (0,)), ((), ()))
 
@@ -80,7 +81,7 @@
         self.first = here.used
         here.used += len(make())
 
-    def copies(self):
+    def copies(self, which):
         return [
             pltpu.make_async_remote_copy(
                 src_ref=src,
@@ -90,15 +91,15 @@
                 device_id=device,
                 device_id_type=MESH,
             )
-            for i, (src, dst, device) in enumerate(self.make())
+            for i, (src, dst, device) in list(enumerate(self.make()))[which]
         ]
 
-    def start(self):
-        for copy in self.copies():
+    def start(self, which=slice(None)):
+        for copy in self.copies(which):
             copy.start()
 
-    def wait(self):
-        for copy in self.copies():
+    def wait(self, which=slice(None)):
+        for copy in self.copies(which):
             copy.wait()
 
 
@@ -109,21 +110,43 @@
 
 
 def gather_slots(here, part):
-    along_z = here.step(
-        lambda: [(part.at[here.slot], part.at[here.slot], here.at(z=z)) for z in here.z_peers()]
-    )
-    along_z.start()
-    yield
-    along_z.wait()
+    forward, back = 1, NX - 1
+
+    def along(x, d):
+        return lax.rem(x + d, NX)
+
+    def slot(x, offset):
+        return part.at[x * NZ + lax.rem(here.z + offset, NZ)]
+
+    def to_z():
+        own = slot(here.x, 0)
+        return [(own, own, here.at(z=lax.rem(here.z + NZ - offset, NZ))) for offset in NEAREST[1:]]
 
     def to_x():
-        own = part.at[pl.ds(here.x * NZ, NZ)]
-        return [(own, own, here.at(x=x)) for x in here.x_peers()]
-
-    along_x = here.step(to_x)
-    along_x.start()
-    yield
-    along_x.wait()
+        blocks = [slot(here.x, offset) for offset in NEAREST]
+        return [(block, block, here.at(x=along(here.x, d))) for block in blocks for d in (forward, back)]
+
+    def to_last():
+        copies = []
+        for i, offset in enumerate(NEAREST):
+            d = (forward, back)[i % 2]
+            block = slot(along(here.x, NX - d), offset)
+            copies.append((block, block, here.at(x=along(here.x, d))))
+        return copies
+
+    z_step, x_step, last_step = here.step(to_z), here.step(to_x), here.step(to_last)
+    z_step.start()
+    x_step.start(slice(0, 2))
+    yield
+    for i in range(1, NZ):
+        z_step.wait(slice(i - 1, i))
+        x_step.start(slice(2 * i, 2 * i + 2))
+    yield
+    for i in range(NZ):
+        x_step.wait(slice(2 * i, 2 * i + 2))
+        last_step.start(slice(i, i + 1))
+    yield
+    last_step.wait()
 
 
 def gather_near(here, ref, skip=0):
@@ -181,23 +204,23 @@
         total = total + from_z[i]
     out[here.u, here.c, chunk(here.x, here.y)] = total
 
-    def to_u():
-        own = out.at[here.u, here.c, chunk(here.x, here.y)]
-        return [(own, own, here.at(u=u)) for u in here.u_peers()]
-
-    along_u = here.step(to_u)
-    along_u.start()
-    yield
-    along_u.wait()
-
-    def to_xy():
-        own = out.at[:, here.c, chunk(here.x, here.y)]
-        return [(own, own, here.at(x=x, y=y)) for x, y in here.xy_peers()]
-
-    across = here.step(to_xy)
-    across.start()
-    yield
-    across.wait()
+    def block(d):
+        return out.at[lax.rem(here.u + d, NU), here.c, chunk(here.x, here.y)]
+
+    near = (1, 3, 2)
+    u_step = here.step(lambda: [(block(0), block(0), here.at(u=lax.rem(here.u + NU - d, NU))) for d in near])
+    xy_step = here.step(
+        lambda: [(block(d), block(d), here.at(x=x, y=y)) for d in (0, *near) for x, y in here.xy_peers()]
+    )
+    peers = NX * NY - 1
+    u_step.start()
+    xy_step.start(slice(0, peers))
+    yield
+    for i in range(1, NU):
+        u_step.wait(slice(i - 1, i))
+        xy_step.start(slice(i * peers, (i + 1) * peers))
+    yield
+    xy_step.wait()
     swap = here.step(lambda: [(out.at[:, here.c], out.at[:, here.c], here.at(c=1 - here.c))])
     swap.start()
     yield
@@ -293,19 +316,17 @@
     ref[at, :] = head
 
 
-def invert(ref, hooks=None):
-    steps = TOTAL // BK
-    if hooks is None:
-
-        def one(k, carry):
-            reduce_block(ref, k, pl.ds(pl.multiple_of(k * BK, BK), BK), lambda: None)
-            return carry
-
-        lax.fori_loop(0, steps, one, 0)
-    else:
-        for k in range(steps):
-            reduce_block(ref, k, pl.ds(k * BK, BK), hooks[2 * k])
-            hooks[2 * k + 1]()
+def invert(ref, hooks=()):
+    peeled = len(hooks) // 2
+    for k in range(peeled):
+        reduce_block(ref, k, pl.ds(k * BK, BK), hooks[2 * k])
+        hooks[2 * k + 1]()
+
+    def one(k, carry):
+        reduce_block(ref, k, pl.ds(pl.multiple_of(k * BK, BK), BK), lambda: None)
+        return carry
+
+    lax.fori_loop(peeled, TOTAL // BK, one, 0)
 
 
 def assemble(gram, ref):
@@ -392,15 +413,34 @@
     with scope("proj1"):
         proj[...] = project(high, feats, here.x, 1)
         proj_low[...] = project(low, feats, here.x, 1)
+    with scope("waithx"):
+        next(gather_high)
+    with scope("proj2"):
+        sides = project(high, feats, here.x + 1, 1) + project(high, feats, here.x + 3, 1)
+        proj[...] = proj[...] + sides
     with scope("m_xy"):
         next(sum_m)
-    with scope("waithx"):
+    with scope("waitlx"):
+        next(gather_low)
+    with scope("waithx2"):
         next(gather_high, None)
-    with scope("proj2"):
-        proj[...] = proj[...] + project(high, feats, here.x + 1, NX - 1)
+    with scope("proj2b"):
+        proj[...] = proj[...] + project(high, feats, here.x + 2, 1)
         t_all[here.u, here.c, :, :count] = proj[...].astype(bf16)
     targets_t = gather_near(here, t_all)
     next(targets_t)
+    with scope("proj3"):
+        sides = project(low, feats, here.x + 1, 1) + project(low, feats, here.x + 3, 1)
+        proj_low[...] = proj_low[...] + sides
+    with scope("waitlx2"):
+        next(gather_low, None)
+    with scope("proj3b"):
+        exact = proj[...] + (proj_low[...] + project(low, feats, here.x + 2, 1))
+        t_err[here.u, here.c, :, :count] = (exact - proj[...].astype(bf16).astype(f32)).astype(bf16)
+    targets_e = gather_near(here, t_err, 1)
+    next(targets_e)
+    with scope("m_z"):
+        next(sum_m)
 
     with scope("image"):
         rounded = proj[...].astype(bf16)
@@ -445,18 +485,7 @@
         q_all[here.u, here.c] = total * (1.0 / total_samples) + RIDGE * b_all[here.u, here.c]
         yield from gather_targets(here, q_all)
 
-    with scope("m_z"):
-        next(sum_m)
-    with scope("waitlx"):
-        next(gather_low, None)
-    with scope("proj3"):
-        exact = proj[...] + (proj_low[...] + project(low, feats, here.x + 1, NX - 1))
-        t_err[here.u, here.c, :, :count] = (exact - proj[...].astype(bf16).astype(f32)).astype(bf16)
-    targets_e = gather_near(here, t_err, 1)
-    next(targets_e)
     image_sum = sum_of_image()
-    with scope("m_u"):
-        next(sum_m)
     with scope("waitt"):
         next(targets_t, None)
     with scope("waite"):
@@ -472,19 +501,21 @@
             share_s[rows] = (quick(value, right, NT) + 0.5 * cross) * (1.0 / total_samples) + RIDGE * share_m[rows]
     sum_s = gram_sum(here, share_s, gram_s, sxy, sz)
     next(sum_s)
+    with scope("m_u"):
+        next(sum_m)
     next(image_sum)
     rest_t = swap_rest(here, t_all)
     next(rest_t)
     with scope("s_xy"):
         next(sum_s)
+    with scope("s_z"):
+        next(sum_s)
     with scope("m_xy2"):
         next(sum_m)
-    with scope("s_z"):
+    with scope("s_u"):
         next(sum_s)
     with scope("image_x"):
         next(image_sum)
-    with scope("s_u"):
-        next(sum_s)
     with scope("m_end"):
         next(sum_m, None)
     with scope("s_xy2"):
@@ -497,17 +528,19 @@
         assemble(gram_sm.at[here.c], mine_inv)
     side, idle = later(image_sum), later()
     with scope("inverse1"):
-        invert(mine_inv, [side, idle, side, idle, side, idle, side, idle])
+        invert(mine_inv, [side, idle, side, idle])
     swap = here.step(lambda: [(inv_sm.at[here.c], inv_sm.at[here.c], here.at(c=1 - here.c))])
     swap.start()
     with scope("drain"):
-        run(rest_b, rest_t, image_sum)
+        next(image_sum)
+        run(rest_b, rest_t)
         assemble(gram_m, m_full)
     with scope("swap"):
         swap.wait()
     with scope("alpha"):
         alpha_t[...] = fine(m_full[...], s_inv[...])
     with scope("resid"):
+        run(image_sum)
         residual = b_all[...].reshape(flat) - fine(alpha_t[...], q_all[...].reshape(flat))
         r_all[...] = residual.reshape(r_all.shape)
         high_r[here.slot] = r_all[here.u, here.c].astype(bf16)
@@ -524,15 +557,19 @@
         next(sum_r)
     with scope("r_gz"):
         next(gather_r)
-    with scope("proj3"):
+    with scope("proj4"):
         proj[...] = project(high_r, feats, here.x, 1)
     with scope("r_z"):
         next(sum_r)
     with scope("r_gx"):
+        next(gather_r)
+    with scope("proj5"):
+        sides = project(high_r, feats, here.x + 1, 1) + project(high_r, feats, here.x + 3, 1)
+        proj[...] = proj[...] + sides
+    with scope("r_gx2"):
         next(gather_r, None)
-    with scope("proj4"):
-        v_own = proj[...] + project(high_r, feats, here.x + 1, NX - 1)
-        v_all[here.u, here.c, :, :count] = v_own.astype(bf16)
+    with scope("proj6"):
+        v_all[here.u, here.c, :, :count] = (proj[...] + project(high_r, feats, here.x + 2, 1)).astype(bf16)
     gather_v = gather_targets(here, v_all)
     next(gather_v)
     with scope("r_u"):

time: 176 us -> 169 us (0.960)
  Pallas kernels: 174 us -> 167 us
    pallas_call x1, Pallas kernels: 174 us -> 167 us  [body(): pl.pallas_call(lambda *refs: kernel(total_samples, *refs), out_shape=jax....]
where the time goes in v4:
time: 169 us
  Pallas kernels  167 us (99%)
    pallas_call x1, Pallas kernels, body(): pl.pallas_call(lambda *refs: kernel(total_samples, *refs), out_shape=jax....  167 us

profile of v4, /device:TPU:1, one launch (start us, length us, event | category | flops | bytes accessed | tf_op | source)
XLA Modules:
  0.0 168.7 jit_solution(8975713140693270072)
XLA Ops:
  0.0 167.3 %cg.1 = f32[64,64]{1,0:T(8,128)} custom-call(bf16[192,128]{1,0:T(8,128)(2,1)} %refs_0_.1, bf16[128,4096]{1,0:T(8,128)(2,1)} %refs_1_.1, f32[1,4096]{1,0:T(1,128)} %bitcast.1, f32[64,64]{1,0:T(8,128)} %refs_3_.1), custom_call_target="tpu_custom_call" | custom-call | tf_op jit(solution)/shard_map/cg/pallas_call | solution.py:638
  167.3 1.4 copy.6
